TPU v7x, 256 devices: a whole 4x4x8 slice. The times are simulated.
256 devices in a mesh: band: 8 (over y, core), fft: 32 (over x, z).
Axes of the slice: x: 4, y: 4, z: 8, core: 2. Of those that a mesh axis runs over, the one named last changes fastest.
Arguments:
- start_bands: float32 [2, 16, 96, 9216], P(None, 'band', 'fft'), may hold values from -6 to 6
- potential: float32 [96, 96, 96], P(None, None, 'fft'), may hold values from -2 to 1
- half_height: int32 [96, 96], P('fft'), may hold values from -1 to 24, as said below
- lower_bound: float32 [1], replicated, may hold values from 1 to 2
- upper_bound: float32 [1], replicated, may hold values from 14 to 16
- fermi_level: float32 [1], replicated, may hold values from 0 to 2
Outputs:
- filtered_bands: float32 [2, 16, 96, 9216], P(None, 'band', 'fft')
- energies: float32 [16], P('band')
- band_energy: float32 [1], replicated
Inputs may be any that keep to these rules, and one draw needn't show every extreme that they name: Column (x, y) keeps exactly the wave vectors whose z frequency f has |f| <= half_height[x, y]; -1 marks an empty column; the column of x = y = 0 holds 24; every column whose x or y frequency exceeds 96/4 in magnitude is empty.
All inputs are finite; a program needn't handle non-finite values.
Results may differ from a plain program's by a relative error of at most 0.0003.
Values sent between devices are 32-bit elements; how exact they have to be, the bound alone decides.
A program may use at most 64 MiB of HBM per device.

v0:
```python
import math

import jax
import jax.numpy as jnp
import ml_dtypes
import numpy as np
from jax import lax
from jax.experimental import pallas as pl
from jax.experimental.pallas import tpu as pltpu
from jax.sharding import PartitionSpec as P

NG = 96
CELLS = float(NG**3)
BOX = 49
KIN = 12.0 / 24**2
TEMPER = 0.5
BANDS = 16
MEMBERS = 16
HOLDERS = 7
ZP = 6
F32, BF16 = jnp.float32, jnp.bfloat16
MESH = pl.DeviceIdType.MESH


def box_frequency():
    r = np.arange(BOX)
    return np.where(r <= 24, r, r - BOX)


def halves(table):
    table = table.astype(np.float32)
    high = table.astype(ml_dtypes.bfloat16)
    low = (table - high.astype(np.float32)).astype(ml_dtypes.bfloat16)
    return high, low


def tables():
    freq = box_frequency()
    angle = 2.0 * math.pi / NG * ((np.arange(NG)[:, None] * freq[None, :]) % NG)
    cosine, sine = np.cos(angle), np.sin(angle)
    ahead = np.zeros((192, 64))
    ahead[:96, :BOX], ahead[96:, :BOX] = cosine, sine
    back = np.zeros((128, 96))
    back[:BOX], back[64 : 64 + BOX] = cosine.T, sine.T
    lanes = np.zeros((128, 256))
    lanes[:BOX, :96], lanes[:BOX, 128:224] = cosine.T, sine.T
    lanes[64 : 64 + BOX, :96], lanes[64 : 64 + BOX, 128:224] = -sine.T, cosine.T
    lanes_back = lanes.T.copy()

    def left(t):
        high, low = halves(t)
        return np.concatenate([high, high, low], axis=1)

    def right(t):
        high, low = halves(t)
        return np.concatenate([high, high, low], axis=0)

    return left(ahead), left(back), right(lanes), right(lanes_back)


def split(x):
    high = x.astype(BF16)
    return high, (x - high.astype(F32)).astype(BF16)


def pieces(x, axis):
    high, low = split(x)
    return jnp.concatenate([high, low, high], axis=axis)


def dot(a, b):
    return jnp.dot(a, b, preferred_element_type=F32)


def dot_t(a, b):
    return lax.dot_general(a, b, (((1,), (1,)), ((), ())), preferred_element_type=F32)


def kernel(
    lower_ref,
    upper_ref,
    xi_ref,
    v_ref,
    ta_ref,
    tb_ref,
    ty_ref,
    tyb_ref,
    out_ref,
    energy_ref,
    xt,
    x0,
    vb,
    cur,
    prev,
    hy,
    inside,
    kin,
    sbuf,
    rbuf,
    bbuf,
    kbuf,
    gy,
    bh,
    bl,
    part,
    col,
    csum,
    full,
    qs,
    ob,
    s_init,
    r_init,
    s_v,
    r_v,
    s_f,
    r_f,
    s_b,
    r_b,
    s_g,
    r_g,
    s_c,
    r_c,
    s_p,
    r_p,
    s_o,
    r_o,
):
    p = lax.axis_index("band")
    i = lax.axis_index("fft")
    y, core = p // 2, p % 2
    gx, gzz = i // 8, i % 8
    gz, zl = gzz // 2, gzz % 2
    band = 4 * y + gz
    chip = 2 * gx + zl
    me = 2 * chip + core
    is_k = jnp.logical_and(core == 1, chip < HOLDERS)
    active = jnp.logical_or(i <= 8, i >= 24)
    lone = i == 8

    def dev(pp, ii):
        return {"band": pp, "fft": ii}

    def member(m):
        return dev(2 * y + m % 2, (m // 4) * 8 + 2 * gz + (m // 2) % 2)

    def holder(b, s):
        return dev(2 * (b // 4) + 1, (s // 2) * 8 + 2 * (b % 4) + s % 2)

    def remote(src, dst, ss, rs, where):
        return pltpu.make_async_remote_copy(
            src_ref=src, dst_ref=dst, send_sem=ss, recv_sem=rs, device_id=where, device_id_type=MESH
        )

    def await_bytes(ref, sem):
        pltpu.make_async_copy(ref, ref, sem).wait()

    lane = lax.broadcasted_iota(jnp.int32, (1, 128), 1)
    sign = jnp.where(lane < 64, -1.0, 1.0).astype(F32)

    def swap(x):
        return pltpu.roll(x, 64, 1)

    for k in range(6):
        xt[k] = xi_ref[k // 3, k % 3].T[:64]

    def kx_of(jj):
        return 3 * i + jj

    for k in range(6):
        j, jj = k // 3, k % 3
        b, kx = 2 * p + j, kx_of(jj)
        valid = jnp.logical_or(kx <= 24, kx >= 72)
        q = jnp.where(kx <= 24, kx, kx - 47)
        s, slot = (q // 8) % 8, q % 8
        s = jnp.minimum(s, HOLDERS - 1)
        target = holder(b, s)
        mine = jnp.logical_and(target["band"] == p, target["fft"] == i)

        @pl.when(jnp.logical_and(valid, mine))
        def _():
            pltpu.make_async_copy(xt.at[k], x0.at[slot], r_init.at[slot]).start()

        @pl.when(jnp.logical_and(valid, jnp.logical_not(mine)))
        def _():
            remote(xt.at[k], x0.at[slot], s_init.at[k], r_init.at[slot], target).start()

    vm, vhalf = i // 2, i % 2

    def v_target(n):
        g = 2 * core + n
        return dev(2 * y + vm % 2, (vm // 4) * 8 + 2 * g + (vm // 2) % 2)

    def v_mine(n):
        t = v_target(n)
        return jnp.logical_and(t["band"] == p, t["fft"] == i)

    for n in range(2):
        dst = vb.at[pl.ds(3 * vhalf, 3)]

        @pl.when(v_mine(n))
        def _():
            pltpu.make_async_copy(v_ref, dst, r_v.at[vhalf]).start()

        @pl.when(jnp.logical_not(v_mine(n)))
        def _():
            remote(v_ref, dst, s_v.at[n], r_v.at[vhalf], v_target(n)).start()

    @pl.when(is_k)
    def _():
        row = lax.broadcasted_iota(jnp.int32, (64, 128), 0)
        col_ = lax.broadcasted_iota(jnp.int32, (64, 128), 1) % 64
        fz = jnp.where(row <= 24, row, row - BOX)
        fy = jnp.where(col_ <= 24, col_, col_ - BOX)
        in_box = jnp.logical_and(row < BOX, col_ < BOX)
        yz = (fz * fz + fy * fy).astype(F32)
        absz = jnp.abs(fz).astype(F32)

        def plane(a, _):
            q = 8 * chip + a

            @pl.when(q < BOX)
            def _():
                await_bytes(x0.at[a], r_init.at[a])
                fx = jnp.where(q <= 24, q, q - BOX)
                data = x0[a]
                height = data[56:57]
                keep = jnp.logical_and(in_box, absz <= height)
                cur[a] = jnp.where(keep, data, 0.0)
                inside[a] = jnp.where(keep, 1.0 / CELLS, 0.0)
                kin[a] = jnp.where(keep, KIN * (yz + (fx * fx).astype(F32)), 0.0)

            @pl.when(q >= BOX)
            def _():
                zero = jnp.zeros((64, 128), F32)
                cur[a] = zero
                inside[a] = zero
                kin[a] = zero

            prev[a] = jnp.zeros((64, 128), F32)
            return 0

        lax.fori_loop(0, 8, plane, 0)

    for h in range(2):
        await_bytes(vb.at[pl.ds(3 * h, 3)], r_v.at[h])

    def forward():
        @pl.when(is_k)
        def _():
            x = jnp.concatenate([cur[a] for a in range(8)], axis=1)
            out = dot(ta_ref[...], pieces(x, 0))
            for a in range(8):
                c, s = out[:96, 128 * a : 128 * a + 128], out[96:, 128 * a : 128 * a + 128]
                sbuf[pl.ds(a, 96, stride=8), :] = c + sign * swap(s)

            def send(m, _):
                src = sbuf.at[pl.ds(pl.multiple_of(48 * m, 8), 48)]

                @pl.when(m == me)
                def _():
                    pltpu.make_async_copy(src, rbuf.at[chip], r_f.at[chip]).start()

                @pl.when(m != me)
                def _():
                    remote(src, rbuf.at[chip], s_f.at[m], r_f.at[chip], member(m)).start()

                return 0

            lax.fori_loop(0, MEMBERS, send, 0)

    def middle():
        for s in range(HOLDERS):
            await_bytes(rbuf.at[s], r_f.at[s])
        zero8 = jnp.zeros((8, 128), F32)
        d = jnp.concatenate(
            [
                jnp.concatenate([rbuf[s, 8 * z : 8 * z + 8, :] for s in range(HOLDERS)] + [zero8], axis=0)
                for z in range(ZP)
            ],
            axis=1,
        )
        out = dot(ta_ref[...], pieces(d, 0))
        planes = [
            out[:96, 128 * z : 128 * z + 128] + sign * swap(out[96:, 128 * z : 128 * z + 128])
            for z in range(ZP)
        ]
        for z in range(ZP):
            psi = dot(pieces(planes[z], 1), ty_ref[...])
            v = vb[z]
            psi = psi * jnp.concatenate([v, v], axis=1)
            planes[z] = dot(pieces(psi, 1), tyb_ref[...])
        out = dot(tb_ref[...], pieces(jnp.concatenate(planes, axis=1), 0))
        for z in range(ZP):
            o = out[:64, 128 * z : 128 * z + 128] - sign * swap(out[64:, 128 * z : 128 * z + 128])
            for s in range(HOLDERS):
                bbuf[s, 8 * z : 8 * z + 8, :] = o[8 * s : 8 * s + 8]

        def send(s, _):
            home = pl.ds(pl.multiple_of(48 * me, 8), 48)
            mine = jnp.logical_and(is_k, s == chip)

            @pl.when(mine)
            def _():
                pltpu.make_async_copy(bbuf.at[s], kbuf.at[home], r_b.at[me]).start()

            @pl.when(jnp.logical_not(mine))
            def _():
                remote(bbuf.at[s], kbuf.at[home], s_b.at[s], r_b.at[me], holder(band, s)).start()

            return 0

        lax.fori_loop(0, HOLDERS, send, 0)

    def backward(finish):
        @pl.when(is_k)
        def _():
            def arrive(m, _):
                await_bytes(kbuf.at[pl.ds(pl.multiple_of(48 * m, 8), 48)], r_b.at[m])
                return 0

            lax.fori_loop(0, MEMBERS, arrive, 0)
            d = jnp.concatenate([kbuf[pl.ds(a, 96, stride=8), :] for a in range(8)], axis=1)
            out = dot(tb_ref[...], pieces(d, 0))
            for a in range(8):
                f = out[:64, 128 * a : 128 * a + 128] - sign * swap(out[64:, 128 * a : 128 * a + 128])
                finish(a, kin[a] * cur[a] + inside[a] * f)

            def sent(m, _):
                @pl.when(m != me)
                def _():
                    await_bytes(sbuf.at[pl.ds(pl.multiple_of(48 * m, 8), 48)], s_f.at[m])

                return 0

            lax.fori_loop(0, MEMBERS, sent, 0)

        def sent_back(s, _):
            @pl.when(jnp.logical_not(jnp.logical_and(is_k, s == chip)))
            def _():
                await_bytes(bbuf.at[s], s_b.at[s])

            return 0

        lax.fori_loop(0, HOLDERS, sent_back, 0)

    center = 0.5 * (upper_ref[0] + lower_ref[0])
    half_width = 0.5 * (upper_ref[0] - lower_ref[0])

    def step(k, _):
        forward()
        middle()
        alpha = jnp.where(k == 0, 1.0, 2.0).astype(F32)
        beta = jnp.where(k == 0, 0.0, 1.0).astype(F32)

        def finish(a, h):
            old = cur[a]
            new = alpha * (h - center * old) / half_width - beta * prev[a]
            prev[a] = old
            cur[a] = new

        backward(finish)
        return 0

    lax.fori_loop(0, 3, step, 0)

    n_planes = jnp.where(chip == HOLDERS - 1, 1, 8)

    def scatter(src, w):
        @pl.when(is_k)
        def _():
            def one(n, _):
                a, t = n // 7, n % 7
                q = 8 * chip + a
                kx = jnp.where(q <= 24, q, q + 47)
                dst = gy.at[w, pl.ds(pl.multiple_of(128 * (kx % 3) + 8 * band, 8), 8)]
                row = src.at[a, pl.ds(pl.multiple_of(8 * t, 8), 8)]
                ii = kx // 3
                mine = jnp.logical_and(t == p, ii == i)

                @pl.when(mine)
                def _():
                    pltpu.make_async_copy(row, dst, r_g.at[w, kx % 3, band]).start()

                @pl.when(jnp.logical_not(mine))
                def _():
                    remote(row, dst, s_g.at[w, n], r_g.at[w, kx % 3, band], dev(t, ii)).start()

                return 0

            lax.fori_loop(0, 7 * n_planes, one, 0)

    def scattered(src, w):
        @pl.when(is_k)
        def _():
            def one(n, _):
                a, t = n // 7, n % 7
                q = 8 * chip + a
                kx = jnp.where(q <= 24, q, q + 47)

                @pl.when(jnp.logical_not(jnp.logical_and(t == p, kx // 3 == i)))
                def _():
                    await_bytes(src.at[a, pl.ds(pl.multiple_of(8 * t, 8), 8)], s_g.at[w, n])

                return 0

            lax.fori_loop(0, 7 * n_planes, one, 0)

    summing = jnp.logical_and(active, p < 7)

    def gather_wait(w):
        def one(n, _):
            jj, b = n // BANDS, n % BANDS
            await_bytes(gy.at[w, pl.ds(pl.multiple_of(128 * jj + 8 * b, 8), 8)], r_g.at[w, jj, b])
            return 0

        lax.fori_loop(0, jnp.where(lone, BANDS, 3 * BANDS), one, 0)

    def rows_of(w):
        out = []
        for jj in range(3):
            for r in range(8):
                x = gy[w, pl.ds(128 * jj + r, BANDS, stride=8), :]
                if jj:
                    x = jnp.where(lone, 0.0, x)
                out.append(x)
        return out

    def with_swapped(rows):
        a = jnp.concatenate(rows, axis=1)
        b = jnp.concatenate([-sign * swap(x) for x in rows], axis=1)
        return jnp.concatenate([a, b], axis=0)

    def partial_sum(w):
        @pl.when(summing)
        def _():
            gather_wait(w)
            high, low = split(with_swapped(rows_of(w)))
            if w == 0:
                bh[...] = high
                bl[...] = low
            g = (
                dot_t(bh[:BANDS], high)
                + dot_t(bh[:BANDS], low)
                + dot_t(bl[:BANDS], high)
            ) * (1.0 / CELLS)
            g = jnp.concatenate([g, jnp.zeros((BANDS, 96), F32)], axis=1)
            part[w] = g
            col[w, p] = g

            def send(t, _):
                @pl.when(t != p)
                def _():
                    remote(part.at[w], col.at[w, p], s_c.at[w, t], r_c.at[w, p], dev(t, i)).start()

                return 0

            lax.fori_loop(0, 8, send, 0)

    slot = jnp.where(i <= 8, i, i - 15)

    def column_sum(w):
        @pl.when(active)
        def _():
            def arrive(t, _):
                @pl.when(t != p)
                def _():
                    await_bytes(col.at[w, t], r_c.at[w, t])

                return 0

            lax.fori_loop(0, 7, arrive, 0)
            total = col[w, 0]
            for t in range(1, 7):
                total = total + col[w, t]
            csum[w] = total
            my_slot = jnp.minimum(jnp.maximum(slot, 0), 16)
            full[w, my_slot] = total

            def send(ii, _):
                @pl.when(ii != i)
                def _():
                    remote(
                        csum.at[w], full.at[w, my_slot], s_p.at[w, ii], r_p.at[w, my_slot], dev(p, ii)
                    ).start()

                return 0

            lax.fori_loop(0, 32, send, 0)

    def total_of(w):
        def arrive(n, _):
            @pl.when(jnp.where(n <= 8, n, n + 15) != i)
            def _():
                await_bytes(full.at[w, n], r_p.at[w, n])

            return 0

        lax.fori_loop(0, 17, arrive, 0)
        total = full[w, 0]
        for n in range(1, 17):
            total = total + full[w, n]
        return total

    lane2 = lax.broadcasted_iota(jnp.int32, (16, 128), 1)

    def embed(g):
        top = jnp.where(lane2 < 16, g, -g)
        bottom = jnp.where(lane2 < 16, pltpu.roll(g, 112, 1), pltpu.roll(g, 16, 1))
        return jnp.where(jnp.concatenate([lane2, lane2], 0) < 32, jnp.concatenate([top, bottom], 0), 0.0)

    def inverse_rows(g):
        row = lax.broadcasted_iota(jnp.int32, (32, 128), 0)
        ln = lax.broadcasted_iota(jnp.int32, (32, 128), 1)
        m = embed(g) + jnp.where(ln == row + 32, 1.0, 0.0)
        for j in range(32):
            pivot = m[j : j + 1, :]
            factor = m[:, j : j + 1] * (1.0 / pivot[:, j : j + 1])
            m = m - jnp.where(row > j, factor, 0.0) * pivot
        diag = jnp.sum(jnp.where(ln == row, m, 0.0), axis=1, keepdims=True)
        u = m[:16] / jnp.sqrt(diag[:16])
        return jnp.where(lane2 < 32, pltpu.roll(u, 96, 1), 0.0)

    scatter(cur, 0)
    forward()
    middle()
    partial_sum(0)

    def keep(a, h):
        hy[a] = h

    backward(keep)
    scatter(hy, 1)
    column_sum(0)
    u = inverse_rows(total_of(0))

    @pl.when(summing)
    def _():
        w2 = jnp.where(lane2 < 16, u, -u)[:, :32]
        w_high, w_low = split(w2)
        q = dot(w_high, bh[...]) + dot(w_high, bl[...]) + dot(w_low, bh[...])
        for n in range(24):
            qs[pl.ds(n, BANDS, stride=24), :] = q[:, 128 * n : 128 * n + 128]

        def send(t, _):
            src = qs.at[pl.ds(pl.multiple_of(48 * t, 8), 48)]

            @pl.when(t == p)
            def _():
                pltpu.make_async_copy(src, ob.at[p], r_o.at[p]).start()

            @pl.when(t != p)
            def _():
                remote(src, ob.at[p], s_o.at[t], r_o.at[p], dev(t, i)).start()

            return 0

        lax.fori_loop(0, 8, send, 0)

    partial_sum(1)
    column_sum(1)

    @pl.when(active)
    def _():
        for t in range(7):
            await_bytes(ob.at[t], r_o.at[t])
        zero = jnp.zeros((72, 128), F32)
        for k in range(6):
            plane = jnp.concatenate([ob[t, 8 * k : 8 * k + 8, :] for t in range(7)] + [zero], axis=0)
            if k % 3:
                plane = jnp.where(lone, 0.0, plane)
            out_ref[k // 3, k % 3] = plane.T

    @pl.when(jnp.logical_not(active))
    def _():
        out_ref[...] = jnp.zeros((2, 3, 128, 128), F32)

    h = embed(total_of(1))
    t = jnp.dot(u[:, :32], h, precision=lax.Precision.HIGHEST, preferred_element_type=F32)
    energy_ref[...] = jnp.broadcast_to(jnp.sum(t * u, axis=1, keepdims=True), (16, 128))

    for k in range(6):
        j, jj = k // 3, k % 3
        kx = kx_of(jj)
        valid = jnp.logical_or(kx <= 24, kx >= 72)
        q = jnp.where(kx <= 24, kx, kx - 47)
        s = jnp.minimum((q // 8) % 8, HOLDERS - 1)
        target = holder(2 * p + j, s)
        mine = jnp.logical_and(target["band"] == p, target["fft"] == i)

        @pl.when(jnp.logical_and(valid, jnp.logical_not(mine)))
        def _():
            await_bytes(xt.at[k], s_init.at[k])

    for n in range(2):

        @pl.when(jnp.logical_not(v_mine(n)))
        def _():
            await_bytes(v_ref, s_v.at[n])

    scattered(cur, 0)
    scattered(hy, 1)
    for w in range(2):

        @pl.when(summing)
        def _():
            def sent(t, _):
                @pl.when(t != p)
                def _():
                    await_bytes(part.at[w], s_c.at[w, t])

                return 0

            lax.fori_loop(0, 8, sent, 0)

        @pl.when(active)
        def _():
            def sent(ii, _):
                @pl.when(ii != i)
                def _():
                    await_bytes(csum.at[w], s_p.at[w, ii])

                return 0

            lax.fori_loop(0, 32, sent, 0)

    @pl.when(summing)
    def _():
        def sent(t, _):
            @pl.when(t != p)
            def _():
                await_bytes(qs.at[pl.ds(pl.multiple_of(48 * t, 8), 48)], s_o.at[t])

            return 0

        lax.fori_loop(0, 8, sent, 0)


def call(lower, upper, xi, v):
    vmem = pl.BlockSpec(memory_space=pltpu.VMEM)
    smem = pl.BlockSpec(memory_space=pltpu.SMEM)
    sem = pltpu.SemaphoreType.DMA

    def buf(*shape):
        return pltpu.VMEM(shape, F32)

    return pl.pallas_call(
        kernel,
        out_shape=(
            jax.ShapeDtypeStruct((2, 3, 128, 128), F32),
            jax.ShapeDtypeStruct((16, 128), F32),
        ),
        in_specs=[smem, smem] + [vmem] * 6,
        out_specs=(vmem, vmem),
        scratch_shapes=[
            buf(6, 64, 128),
            buf(8, 64, 128),
            buf(6, 96, 128),
            buf(8, 64, 128),
            buf(8, 64, 128),
            buf(8, 64, 128),
            buf(8, 64, 128),
            buf(8, 64, 128),
            buf(768, 128),
            buf(7, 48, 128),
            buf(7, 48, 128),
            buf(768, 128),
            buf(2, 384, 128),
            pltpu.VMEM((32, 3072), BF16),
            pltpu.VMEM((32, 3072), BF16),
            buf(2, 16, 128),
            buf(2, 8, 16, 128),
            buf(2, 16, 128),
            buf(2, 17, 16, 128),
            buf(384, 128),
            buf(7, 48, 128),
            sem((6,)),
            sem((8,)),
            sem((2,)),
            sem((2,)),
            sem((16,)),
            sem((7,)),
            sem((7,)),
            sem((16,)),
            sem((2, 56)),
            sem((2, 3, 16)),
            sem((2, 8)),
            sem((2, 8)),
            sem((2, 32)),
            sem((2, 17)),
            sem((8,)),
            sem((7,)),
        ],
        compiler_params=pltpu.CompilerParams(has_side_effects=True, vmem_limit_bytes=48 * 2**20),
    )(lower, upper, xi, v, *[jnp.asarray(t) for t in tables()])


def boxed(x, axis):
    index = [slice(None)] * x.ndim
    index[axis] = slice(0, 25)
    low = x[tuple(index)]
    index[axis] = slice(72, 96)
    return jnp.concatenate([low, x[tuple(index)]], axis=axis)


def unboxed(x, axis):
    index = [slice(None)] * x.ndim
    index[axis] = slice(0, 25)
    low = x[tuple(index)]
    index[axis] = slice(25, 49)
    high = x[tuple(index)]
    shape = list(x.shape)
    shape[axis] = 47
    return jnp.concatenate([low, jnp.zeros(shape, x.dtype), high], axis=axis)


def local(start_bands, potential, half_height, lower_bound, upper_bound, fermi_level):
    x = start_bands.reshape(2, 2, 3, NG, NG)
    x = boxed(boxed(x, 3), 4)
    x = jnp.pad(x, ((0, 0), (0, 0), (0, 0), (0, 15), (0, 7)))
    height = jnp.pad(boxed(half_height, 1), ((0, 0), (0, 15)), constant_values=-1).astype(F32)
    height = jnp.broadcast_to(height[None, None, :, :, None], (2, 2, 3, 64, 1))
    x = jnp.concatenate([x, height, jnp.zeros((2, 2, 3, 64, 71), F32)], axis=4)
    xi = x.transpose(1, 2, 0, 3, 4).reshape(2, 3, 128, 128)
    v = jnp.pad(potential.transpose(2, 0, 1), ((0, 0), (0, 0), (0, 32)))
    out, energy = call(lower_bound, upper_bound, xi, v)
    q = out.reshape(2, 3, 2, 64, 128)[:, :, :, :BOX, :BOX].transpose(2, 0, 1, 3, 4)
    bands = unboxed(unboxed(q, 3), 4).reshape(2, 2, 3, NG * NG)
    energies = energy[:, 0]
    own = lax.dynamic_slice_in_dim(energies, 2 * lax.axis_index("band"), 2, 0)
    weights = jax.nn.sigmoid((fermi_level[0] - energies) / TEMPER)
    band_energy = (jnp.sum(weights * energies) / float(BANDS)).reshape(1)
    return bands, own, band_energy


def solution(mesh):
    placed = (P(None, "band", "fft", None), P(None, None, "fft"), P("fft", None), P(), P(), P())
    return jax.shard_map(
        local,
        mesh=mesh,
        in_specs=placed,
        out_specs=(P(None, "band", "fft", None), P("band"), P()),
        check_vma=False,
    )
```

profile of v0, /device:TPU:1, one launch (start us, length us, event | category | flops | bytes accessed | tf_op | source)
XLA Modules:
  0.0 131.0 jit_solution(9559482004914652250)
XLA Ops:
  2.6 0.1 pad.23.clone
  2.7 0.1 pad.19.clone
  2.8 0.8 slice.41
  3.6 0.8 pad_add_fusion
  4.3 0.9 pad.14.v_ref
  5.2 0.1 broadcast_in_dim.15
  5.4 0.4 reshape.25
  5.8 0.2 pad_maximum_fusion.2
  6.0 0.2 select_maximum_fusion
  6.2 0.0 copy-start
  6.2 0.0 copy-start.1
  6.2 0.2 maximum_maximum_fusion
  6.4 0.7 copy-done
  7.1 0.1 copy-done.1
  7.2 0.1 copy-done.2
  7.3 0.0 copy-done.3
  7.3 118.6 %shard_map.121 = (f32[2,3,128,128]{3,2,1,0:T(8,128)S(1)}, f32[16,128]{1,0:T(8,128)S(1)}) custom-call(f32[1]{0:T(128)S(6)} %copy.34.lower_ref, f32[1]{0:T(128)S(6)} %copy.35.upper_ref, f32[2,3,128,128]{3,2,1,0:T(8,128)S(1)} %bitcast.18, f32[3,96,128]{2,1,0:T(8,128)S(1)} %pad.14.v_ref, bf16[192,192]{1,0:T(8,128)(2,1)S(1)} %copy-done.3, ...), custom_call_target="tpu_custom_call" | custom-call | tf_op jit(solution)/shard_map/pallas_call | solution.py:646
  125.9 0.1 slice_reduce_fusion
  126.1 0.6 fusion
  127.3 0.6 dynamic-slice_reduce_fusion
  128.0 0.1 pad_maximum_fusion
  128.1 0.2 slice.56
  128.3 0.2 pad_maximum_fusion.1
  128.5 1.4 %reshape.28 = f32[2,2,3,9216]{3,1,2,0:T(2,128)} reshape(f32[2,2,3,96,96]{4,3,1,2,0:T(8,128)S(1)} %pad_maximum_fusion.1) | data formatting | bytes 884736 | tf_op jit(solution)/shard_map/reshape | solution.py:727
  (10 shorter events, 0.1 us)
Async XLA Ops:
  0.6 4.7 %copy-start.4 = (f32[2,2,3,9216]{3,1,2,0:T(2,128)S(1)}, f32[2,2,3,9216]{3,1,2,0:T(2,128)}, u32[]{:S(2)}) copy-start(f32[2,2,3,9216]{3,1,2,0:T(2,128)} %param.10) | copy-start | bytes 1327108
  6.2 0.9 copy-start
  6.2 1.0 copy-start.1
  6.2 1.1 copy-start.2
  6.2 1.1 copy-start.3
where the time goes:
time: 131 us
  Pallas kernels  119 us (91%)
  local copies, waits for them, and re-layouts  5.69 us (4%)
  between operations  4.54 us (3%)
  other arithmetic  2.23 us (2%)
    pallas_call x1, Pallas kernels, call(): pl.pallas_call(kernel, out_shape=(jax.ShapeDtypeStruct((2, 3, 128, 128),...  119 us

commit v1 on v0

v1 whole, which is shorter than its diff:
```python
import math

import jax
import jax.numpy as jnp
import ml_dtypes
import numpy as np
from jax import lax
from jax.experimental import pallas as pl
from jax.experimental.pallas import tpu as pltpu
from jax.sharding import PartitionSpec as P

NG = 96
CELLS = float(NG**3)
BOX = 49
KIN = 12.0 / 24**2
TEMPER = 0.5
BANDS = 16
MEMBERS = 16
HOLDERS = 7
ZP = 3
F32, BF16 = jnp.float32, jnp.bfloat16
MESH = pl.DeviceIdType.MESH


def box_frequency():
    r = np.arange(BOX)
    return np.where(r <= 24, r, r - BOX)


def halves(table):
    table = table.astype(np.float32)
    high = table.astype(ml_dtypes.bfloat16)
    low = (table - high.astype(np.float32)).astype(ml_dtypes.bfloat16)
    return high, low


def tables():
    freq = box_frequency()
    angle = 2.0 * math.pi / NG * ((np.arange(NG)[:, None] * freq[None, :]) % NG)
    cosine, sine = np.cos(angle), np.sin(angle)
    ahead = np.zeros((192, 64))
    ahead[:96, :BOX], ahead[96:, :BOX] = cosine, sine
    back = np.zeros((128, 96))
    back[:BOX], back[64 : 64 + BOX] = cosine.T, sine.T
    lanes = np.zeros((128, 256))
    lanes[:BOX, :96], lanes[:BOX, 128:224] = cosine.T, sine.T
    lanes[64 : 64 + BOX, :96], lanes[64 : 64 + BOX, 128:224] = -sine.T, cosine.T
    lanes_back = lanes.T.copy()
    plane = np.arange(NG).reshape(MEMBERS, 2, ZP)

    def left(t):
        high, low = halves(t)
        return np.concatenate([high, high, low], axis=1)

    def right(t):
        high, low = halves(t)
        return np.concatenate([high, high, low], axis=0)

    z_ahead = [np.concatenate([ahead[plane[:, h].ravel()], ahead[96 + plane[:, h].ravel()]]) for h in range(2)]
    z_back = [back[:, plane[:, h].ravel()] for h in range(2)]
    return (
        np.stack([left(t) for t in z_ahead]),
        left(ahead),
        np.stack([left(t) for t in z_back]),
        left(back),
        right(lanes),
        right(lanes_back),
    )


def split(x):
    high = x.astype(BF16)
    return high, (x - high.astype(F32)).astype(BF16)


def pieces(x, axis):
    high, low = split(x)
    return jnp.concatenate([high, low, high], axis=axis)


def dot(a, b):
    return jnp.dot(a, b, preferred_element_type=F32)


def dot_t(a, b):
    return lax.dot_general(a, b, (((1,), (1,)), ((), ())), preferred_element_type=F32)


def kernel(
    lower_ref,
    upper_ref,
    fermi_ref,
    height_ref,
    x_hbm,
    v_hbm,
    tz_hbm,
    tx_hbm,
    tzb_hbm,
    txb_hbm,
    ty_hbm,
    tyb_hbm,
    out_hbm,
    energy_ref,
    band_energy_ref,
    xin,
    grid,
    tz,
    tx,
    tzb,
    txb,
    ty,
    tyb,
    xt,
    x0,
    vb,
    cur,
    prev,
    hy,
    inside,
    kin,
    sbuf,
    rbuf,
    bbuf,
    kbuf,
    gy,
    bh,
    bl,
    part,
    col,
    csum,
    full,
    epart,
    ecol,
    ecsum,
    efull,
    qs,
    ob,
    s_in,
    s_out,
    s_t,
    s_init,
    r_init,
    s_v,
    r_v,
    s_f,
    r_f,
    s_b,
    r_b,
    s_g,
    r_g,
    s_c,
    r_c,
    s_p,
    r_p,
    s_o,
    r_o,
    planes_in,
):
    p = lax.axis_index("band")
    i = lax.axis_index("fft")
    y, core = p // 2, p % 2
    y2, yl = y // 2, y % 2
    gx, gzz = i // 8, i % 8
    x2, xl = gx // 2, gx % 2
    gz, zl = gzz // 2, gzz % 2
    band = 8 * y2 + 4 * x2 + gz
    chip = 4 * yl + 2 * xl + zl
    me = 2 * chip + core
    is_k = jnp.logical_and(core == 1, chip < HOLDERS)
    active = jnp.logical_or(i <= 8, i >= 24)
    lone = i == 8
    summing = jnp.logical_and(active, p < 7)

    def dev(pp, ii):
        return {"band": pp, "fft": ii}

    def member_of(b, m):
        c = m // 2
        return dev(
            2 * (2 * (b // 8) + c // 4) + m % 2,
            (2 * ((b // 4) % 2) + (c // 2) % 2) * 8 + 2 * (b % 4) + c % 2,
        )

    def holder(b, s):
        return member_of(b, 2 * s + 1)

    def is_me(where):
        return jnp.logical_and(where["band"] == p, where["fft"] == i)

    def remote(src, dst, ss, rs, where):
        return pltpu.make_async_remote_copy(
            src_ref=src, dst_ref=dst, send_sem=ss, recv_sem=rs, device_id=where, device_id_type=MESH
        )

    def await_bytes(ref, sem):
        pltpu.make_async_copy(ref, ref, sem).wait()

    barrier = pltpu.get_barrier_semaphore()
    here = (p % 4) * 32 + i

    def greet(n, _):
        at = (here + n) % 128
        pl.semaphore_signal(barrier, inc=1, device_id=dev(4 * (p // 4) + at // 32, at % 32), device_id_type=MESH)
        return 0

    def others(n):
        return dev(4 * (1 - p // 4) + n, i)

    pltpu.make_async_copy(x_hbm, xin, s_in.at[0]).start()
    for n, (src, dst) in enumerate(
        ((tz_hbm, tz), (tx_hbm, tx), (tzb_hbm, tzb), (txb_hbm, txb), (ty_hbm, ty), (tyb_hbm, tyb))
    ):
        pltpu.make_async_copy(src, dst, s_t.at[n]).start()
    lax.fori_loop(1, 128, greet, 0)
    for n in range(4):
        pl.semaphore_signal(barrier, inc=1, device_id=others(n), device_id_type=MESH)

    lane = lax.broadcasted_iota(jnp.int32, (1, 128), 1)
    sign = jnp.where(lane < 64, -1.0, 1.0).astype(F32)

    def swap(x):
        return pltpu.roll(x, 64, 1)

    def boxed_lanes(x):
        return jnp.where(lane < 25, x, jnp.where(lane < BOX, pltpu.roll(x, 128 - 47, 1), 0.0))

    await_bytes(xin, s_in.at[0])
    for k in range(6):
        j, jj = k // 3, k % 3
        for c in range(2):
            t0, t1, t2 = (xin[3 * c + jj, pl.ds(2 * t + j, 24, stride=6), :] for t in range(3))
            quarter = (
                t0,
                jnp.where(lane < 32, pltpu.roll(t0, 32, 1), pltpu.roll(t1, 32, 1)),
                jnp.where(lane < 64, pltpu.roll(t1, 64, 1), pltpu.roll(t2, 64, 1)),
                pltpu.roll(t2, 96, 1),
            )
            for r in range(4):
                grid[c, pl.ds(r, 24, stride=4), :] = boxed_lanes(quarter[r])
        pad = jnp.zeros((15, 128), F32)
        rows = jnp.concatenate([grid[0, 0:25], grid[0, 72:96], pad, grid[1, 0:25], grid[1, 72:96], pad], axis=0)
        xt[k] = rows.T[:64]
    for jj in range(3):
        h = height_ref[jj : jj + 1, :].astype(F32)
        h = boxed_lanes(jnp.concatenate([h, jnp.zeros((1, 32), F32)], axis=1))
        h = jnp.where(lane < BOX, h, -1.0)
        h = jnp.where(lane < 64, h, pltpu.roll(h, 64, 1))
        for j in range(2):
            xt[3 * j + jj, 56:57, :] = h

    pl.semaphore_wait(barrier, 131)
    for n in range(4):
        pl.semaphore_signal(planes_in, inc=1, device_id=others(n), device_id_type=MESH)

    def start_of(k):
        j, jj = k // 3, k % 3
        kx = 3 * i + jj
        valid = jnp.logical_or(kx <= 24, kx >= 72)
        q = jnp.where(kx <= 24, kx, kx - 47)
        s = jnp.minimum((q // 8) % 8, HOLDERS - 1)
        return valid, q % 8, holder(2 * p + j, s)

    for k in range(6):
        valid, slot, target = start_of(k)

        @pl.when(jnp.logical_and(valid, is_me(target)))
        def _():
            pltpu.make_async_copy(xt.at[k], x0.at[slot], r_init.at[slot]).start()

        @pl.when(jnp.logical_and(valid, jnp.logical_not(is_me(target))))
        def _():
            remote(xt.at[k], x0.at[slot], s_init.at[k], r_init.at[slot], target).start()

    gives_v = jnp.logical_and(core == 0, yl == i // 16)

    @pl.when(gives_v)
    def _():
        def one(g, _):
            target = member_of(8 * y2 + g, i // 2)
            dst = vb.at[pl.ds(3 * (i % 2), 3)]

            @pl.when(is_me(target))
            def _():
                pltpu.make_async_copy(v_hbm, dst, r_v.at[i % 2]).start()

            @pl.when(jnp.logical_not(is_me(target)))
            def _():
                remote(v_hbm, dst, s_v.at[g], r_v.at[i % 2], target).start()

            return 0

        lax.fori_loop(0, 8, one, 0)

    for n, dst in enumerate((tz, tx, tzb, txb, ty, tyb)):
        await_bytes(dst, s_t.at[n])

    @pl.when(is_k)
    def _():
        row = lax.broadcasted_iota(jnp.int32, (64, 128), 0)
        col_ = lax.broadcasted_iota(jnp.int32, (64, 128), 1) % 64
        fz = jnp.where(row <= 24, row, row - BOX)
        fy = jnp.where(col_ <= 24, col_, col_ - BOX)
        in_box = jnp.logical_and(row < BOX, col_ < BOX)
        yz = (fz * fz + fy * fy).astype(F32)
        absz = jnp.abs(fz).astype(F32)

        def plane(a, _):
            q = 8 * chip + a

            @pl.when(q < BOX)
            def _():
                await_bytes(x0.at[a], r_init.at[a])
                fx = jnp.where(q <= 24, q, q - BOX)
                data = x0[a]
                height = data[56:57]
                keep = jnp.logical_and(in_box, absz <= height)
                cur[a] = jnp.where(keep, data, 0.0)
                inside[a] = jnp.where(keep, 1.0 / CELLS, 0.0)
                kin[a] = jnp.where(keep, KIN * (yz + (fx * fx).astype(F32)), 0.0)

            @pl.when(q >= BOX)
            def _():
                zero = jnp.zeros((64, 128), F32)
                cur[a] = zero
                inside[a] = zero
                kin[a] = zero

            prev[a] = jnp.zeros((64, 128), F32)
            return 0

        lax.fori_loop(0, 8, plane, 0)

    def message(m):
        return pl.ds(pl.multiple_of(24 * m, 8), 24)

    def forward():
        @pl.when(is_k)
        def _():
            x = pieces(jnp.concatenate([cur[a] for a in range(8)], axis=1), 0)
            for h in range(2):
                out = dot(tz[h], x)
                for a in range(8):
                    c, s = out[:48, 128 * a : 128 * a + 128], out[48:, 128 * a : 128 * a + 128]
                    sbuf[h, pl.ds(a, 48, stride=8), :] = c + sign * swap(s)

                def send(m, _):
                    src = sbuf.at[h, message(m)]

                    @pl.when(m == me)
                    def _():
                        pltpu.make_async_copy(src, rbuf.at[h, chip], r_f.at[h, chip]).start()

                    @pl.when(m != me)
                    def _():
                        remote(
                            src, rbuf.at[h, chip], s_f.at[h, m], r_f.at[h, chip], member_of(band, m)
                        ).start()

                    return 0

                lax.fori_loop(0, MEMBERS, send, 0)

    def middle(first):
        zero8 = jnp.zeros((8, 128), F32)
        zero32 = jnp.zeros((288, 32), F32)
        for h in range(2):
            for s in range(HOLDERS):
                await_bytes(rbuf.at[h, s], r_f.at[h, s])
            d = jnp.concatenate(
                [
                    jnp.concatenate(
                        [rbuf[h, s, 8 * z : 8 * z + 8, :] for s in range(HOLDERS)] + [zero8], axis=0
                    )
                    for z in range(ZP)
                ],
                axis=1,
            )
            out = dot(tx[...], pieces(d, 0))
            rows = jnp.concatenate(
                [
                    out[:96, 128 * z : 128 * z + 128] + sign * swap(out[96:, 128 * z : 128 * z + 128])
                    for z in range(ZP)
                ],
                axis=0,
            )
            psi = dot(pieces(rows, 1), ty[...])

            @pl.when(first)
            def _():
                await_bytes(vb.at[pl.ds(3 * h, 3)], r_v.at[h])

            v = jnp.concatenate([vb[3 * h + z] for z in range(ZP)], axis=0)
            v = jnp.concatenate([v, zero32], axis=1)
            psi = psi * jnp.concatenate([v, v], axis=1)
            rows = dot(pieces(psi, 1), tyb[...])
            d = jnp.concatenate([rows[96 * z : 96 * z + 96] for z in range(ZP)], axis=1)
            out = dot(txb[...], pieces(d, 0))
            for z in range(ZP):
                o = out[:64, 128 * z : 128 * z + 128] - sign * swap(out[64:, 128 * z : 128 * z + 128])
                for s in range(HOLDERS):
                    bbuf[h, s, 8 * z : 8 * z + 8, :] = o[8 * s : 8 * s + 8]

            def send(s, _):
                home = kbuf.at[h, message(me)]
                mine = jnp.logical_and(is_k, s == chip)

                @pl.when(mine)
                def _():
                    pltpu.make_async_copy(bbuf.at[h, s], home, r_b.at[h, me]).start()

                @pl.when(jnp.logical_not(mine))
                def _():
                    remote(bbuf.at[h, s], home, s_b.at[h, s], r_b.at[h, me], holder(band, s)).start()

                return 0

            lax.fori_loop(0, HOLDERS, send, 0)

    def backward(finish):
        @pl.when(is_k)
        def _():
            out = None
            for h in range(2):

                def arrive(m, _):
                    await_bytes(kbuf.at[h, message(m)], r_b.at[h, m])
                    return 0

                lax.fori_loop(0, MEMBERS, arrive, 0)
                d = jnp.concatenate([kbuf[h, pl.ds(a, 48, stride=8), :] for a in range(8)], axis=1)
                term = dot(tzb[h], pieces(d, 0))
                out = term if out is None else out + term
            for a in range(8):
                f = out[:64, 128 * a : 128 * a + 128] - sign * swap(out[64:, 128 * a : 128 * a + 128])
                finish(a, kin[a] * cur[a] + inside[a] * f)

            for h in range(2):

                def sent(m, _):
                    @pl.when(m != me)
                    def _():
                        await_bytes(sbuf.at[h, message(m)], s_f.at[h, m])

                    return 0

                lax.fori_loop(0, MEMBERS, sent, 0)

        for h in range(2):

            def sent_back(s, _):
                @pl.when(jnp.logical_not(jnp.logical_and(is_k, s == chip)))
                def _():
                    await_bytes(bbuf.at[h, s], s_b.at[h, s])

                return 0

            lax.fori_loop(0, HOLDERS, sent_back, 0)

    center = 0.5 * (upper_ref[0] + lower_ref[0])
    half_width = 0.5 * (upper_ref[0] - lower_ref[0])

    def step(k, _):
        forward()
        middle(k == 0)
        alpha = jnp.where(k == 0, 1.0, 2.0).astype(F32)
        beta = jnp.where(k == 0, 0.0, 1.0).astype(F32)

        def finish(a, h):
            old = cur[a]
            new = alpha * (h - center * old) / half_width - beta * prev[a]
            prev[a] = old
            cur[a] = new

        backward(finish)
        return 0

    lax.fori_loop(0, 3, step, 0)

    n_planes = jnp.where(chip == HOLDERS - 1, 1, 8)

    def row_of(n):
        a, t = n // 7, n % 7
        q = 8 * chip + a
        return a, t, jnp.where(q <= 24, q, q + 47)

    def scatter(src, w):
        @pl.when(is_k)
        def _():
            def one(n, _):
                a, t, kx = row_of(n)
                dst = gy.at[w, pl.ds(pl.multiple_of(128 * (kx % 3) + 8 * band, 8), 8)]
                row = src.at[a, pl.ds(pl.multiple_of(8 * t, 8), 8)]
                target = dev(t, kx // 3)

                @pl.when(is_me(target))
                def _():
                    pltpu.make_async_copy(row, dst, r_g.at[w, kx % 3, band]).start()

                @pl.when(jnp.logical_not(is_me(target)))
                def _():
                    remote(row, dst, s_g.at[w, n], r_g.at[w, kx % 3, band], target).start()

                return 0

            lax.fori_loop(0, 7 * n_planes, one, 0)

    def scattered(src, w):
        @pl.when(is_k)
        def _():
            def one(n, _):
                a, t, kx = row_of(n)

                @pl.when(jnp.logical_not(is_me(dev(t, kx // 3))))
                def _():
                    await_bytes(src.at[a, pl.ds(pl.multiple_of(8 * t, 8), 8)], s_g.at[w, n])

                return 0

            lax.fori_loop(0, 7 * n_planes, one, 0)

    def all_rows(w):
        def one(n, _):
            jj, b = n // BANDS, n % BANDS
            await_bytes(gy.at[w, pl.ds(pl.multiple_of(128 * jj + 8 * b, 8), 8)], r_g.at[w, jj, b])
            return 0

        lax.fori_loop(0, jnp.where(lone, BANDS, 3 * BANDS), one, 0)
        rows = []
        for jj in range(3):
            for r in range(8):
                x = gy[w, pl.ds(128 * jj + r, BANDS, stride=8), :]
                rows.append(jnp.where(lone, 0.0, x) if jj else x)
        a = jnp.concatenate(rows, axis=1)
        b = jnp.concatenate([-sign * swap(x) for x in rows], axis=1)
        return jnp.concatenate([a, b], axis=0)

    my_slot = jnp.minimum(jnp.where(i <= 8, i, jnp.maximum(i - 15, 0)), 16)

    def slot_fft(n):
        return jnp.where(n <= 8, n, n + 15)

    def column_send(w, mine, theirs):
        def send(t, _):
            @pl.when(t != p)
            def _():
                remote(mine, theirs.at[p], s_c.at[w, t], r_c.at[w, p], dev(t, i)).start()

            return 0

        lax.fori_loop(0, 8, send, 0)

    def column_sum(w, theirs):
        def arrive(t, _):
            @pl.when(t != p)
            def _():
                await_bytes(theirs.at[t], r_c.at[w, t])

            return 0

        lax.fori_loop(0, 7, arrive, 0)
        total = theirs[0]
        for t in range(1, 7):
            total = total + theirs[t]
        return total

    def plane_send(w, mine, theirs, count, fft_of):
        def send(n, _):
            ii = fft_of(n)

            @pl.when(ii != i)
            def _():
                remote(mine, theirs.at[my_slot], s_p.at[w, n], r_p.at[w, my_slot], dev(p, ii)).start()

            return 0

        lax.fori_loop(0, count, send, 0)

    def plane_sum(w, theirs):
        def arrive(n, _):
            @pl.when(slot_fft(n) != i)
            def _():
                await_bytes(theirs.at[n], r_p.at[w, n])

            return 0

        lax.fori_loop(0, 17, arrive, 0)
        total = theirs[0]
        for n in range(1, 17):
            total = total + theirs[n]
        return total

    lane2 = lax.broadcasted_iota(jnp.int32, (16, 128), 1)

    def inverse_rows(g):
        row = lax.broadcasted_iota(jnp.int32, (32, 128), 0)
        ln = lax.broadcasted_iota(jnp.int32, (32, 128), 1)
        top = jnp.where(lane2 < 16, g, -g)
        bottom = jnp.where(lane2 < 16, pltpu.roll(g, 112, 1), pltpu.roll(g, 16, 1))
        m = jnp.where(ln < 32, jnp.concatenate([top, bottom], 0), 0.0)
        m = m + jnp.where(ln == row + 32, 1.0, 0.0)
        for j in range(32):
            pivot = m[j : j + 1, :]
            factor = m[:, j : j + 1] * (1.0 / pivot[:, j : j + 1])
            m = m - jnp.where(row > j, factor, 0.0) * pivot
        diag = jnp.sum(jnp.where(ln == row, m, 0.0), axis=1, keepdims=True)
        u = m[:16] / jnp.sqrt(diag[:16])
        return jnp.where(lane2 < 32, pltpu.roll(u, 96, 1), 0.0)

    forward()
    pl.semaphore_wait(planes_in, 4)
    scatter(cur, 0)
    middle(False)

    @pl.when(summing)
    def _():
        high, low = split(all_rows(0))
        bh[...] = high
        bl[...] = low
        g = (dot_t(bh[:BANDS], high) + dot_t(bh[:BANDS], low) + dot_t(bl[:BANDS], high)) * (1.0 / CELLS)
        g = jnp.concatenate([g, jnp.zeros((BANDS, 96), F32)], axis=1)
        packed = g[0:4]
        for n in range(1, 4):
            packed = packed + pltpu.roll(g[4 * n : 4 * n + 4], 32 * n, 1)
        part[...] = packed
        col[p] = packed
        column_send(0, part, col)

    @pl.when(active)
    def _():
        total = column_sum(0, col)
        csum[...] = total
        full[my_slot] = total
        plane_send(0, csum, full, 17, slot_fft)

    def keep(a, h):
        hy[a] = h

    backward(keep)
    scatter(hy, 1)

    @pl.when(active)
    def _():
        total = plane_sum(0, full)

        @pl.when(p < 7)
        def _():
            g = jnp.concatenate([total] + [pltpu.roll(total, 128 - 32 * n, 1) for n in range(1, 4)], axis=0)
            u = inverse_rows(jnp.where(lane2 < 32, g, 0.0))
            w_high, w_low = split(jnp.where(lane2 < 16, u, -u)[:, :32])

            def rotated(high, low):
                return dot(w_high, high) + dot(w_high, low) + dot(w_low, high)

            q = rotated(bh[...], bl[...])
            for n in range(24):
                qs[pl.ds(n, BANDS, stride=24), :] = q[:, 128 * n : 128 * n + 128]

            def send(t, _):
                src = qs.at[pl.ds(pl.multiple_of(48 * t, 8), 48)]

                @pl.when(t == p)
                def _():
                    pltpu.make_async_copy(src, ob.at[p], r_o.at[p]).start()

                @pl.when(t != p)
                def _():
                    remote(src, ob.at[p], s_o.at[t], r_o.at[p], dev(t, i)).start()

                return 0

            lax.fori_loop(0, 8, send, 0)
            hq = rotated(*split(all_rows(1)))
            e = q[:, :128] * hq[:, :128]
            for n in range(1, 24):
                e = e + q[:, 128 * n : 128 * n + 128] * hq[:, 128 * n : 128 * n + 128]
            e = jnp.sum(e, axis=1, keepdims=True) * (1.0 / CELLS)
            row = lax.broadcasted_iota(jnp.int32, (16, 128), 0)
            e = jnp.sum(jnp.where(lane2 == row, e, 0.0), axis=0, keepdims=True)
            epart[...] = e
            ecol[p] = e
            column_send(1, epart, ecol)

        total = column_sum(1, ecol)
        ecsum[...] = total
        efull[my_slot] = total
        plane_send(1, ecsum, efull, 32, lambda n: n)

        for t in range(7):
            await_bytes(ob.at[t], r_o.at[t])
        zero = jnp.zeros((72, 128), F32)
        low_lanes, high_lanes = lane < 25, jnp.logical_and(lane >= 72, lane < 96)
        for k in range(6):
            j, jj = k // 3, k % 3
            rows = jnp.concatenate([ob[t, 8 * k : 8 * k + 8, :] for t in range(7)] + [zero], axis=0)
            if jj:
                rows = jnp.where(lone, 0.0, rows)
            rows = rows.T
            rows = jnp.where(low_lanes, rows, jnp.where(high_lanes, pltpu.roll(rows, 47, 1), 0.0))
            for c in range(2):
                grid[c, 0:25] = rows[64 * c : 64 * c + 25]
                grid[c, 25:72] = jnp.zeros((47, 128), F32)
                grid[c, 72:96] = rows[64 * c + 25 : 64 * c + BOX]
                o0, o1, o2, o3 = (grid[c, pl.ds(r, 24, stride=4), :] for r in range(4))
                thirds = (
                    jnp.where(lane < 96, o0, pltpu.roll(o1, 96, 1)),
                    jnp.where(lane < 64, pltpu.roll(o1, 96, 1), pltpu.roll(o2, 64, 1)),
                    jnp.where(lane < 32, pltpu.roll(o2, 64, 1), pltpu.roll(o3, 32, 1)),
                )
                for t in range(3):
                    xin[3 * c + jj, pl.ds(2 * t + j, 24, stride=6), :] = thirds[t]

    @pl.when(jnp.logical_not(active))
    def _():
        xin[...] = jnp.zeros((6, 144, 128), F32)

    pltpu.make_async_copy(xin, out_hbm, s_out.at[0]).start()
    e = plane_sum(1, efull)
    for j in range(2):
        energy_ref[j] = jnp.sum(jnp.where(lane == 2 * p + j, e, 0.0))
    weights = jax.nn.sigmoid((fermi_ref[0] - e) / TEMPER)
    band_energy_ref[0] = jnp.sum(jnp.where(lane < BANDS, weights * e, 0.0)) / float(BANDS)

    for k in range(6):
        valid, _, target = start_of(k)

        @pl.when(jnp.logical_and(valid, jnp.logical_not(is_me(target))))
        def _():
            await_bytes(xt.at[k], s_init.at[k])

    @pl.when(gives_v)
    def _():
        def one(g, _):
            @pl.when(jnp.logical_not(is_me(member_of(8 * y2 + g, i // 2))))
            def _():
                await_bytes(v_hbm, s_v.at[g])

            return 0

        lax.fori_loop(0, 8, one, 0)

    scattered(cur, 0)
    scattered(hy, 1)
    for w, (mine, mine2) in enumerate(((part, csum), (epart, ecsum))):

        @pl.when(summing)
        def _():
            def sent(t, _):
                @pl.when(t != p)
                def _():
                    await_bytes(mine, s_c.at[w, t])

                return 0

            lax.fori_loop(0, 8, sent, 0)

        @pl.when(active)
        def _():
            def sent(n, _):
                @pl.when((n if w else slot_fft(n)) != i)
                def _():
                    await_bytes(mine2, s_p.at[w, n])

                return 0

            lax.fori_loop(0, 32 if w else 17, sent, 0)

    @pl.when(summing)
    def _():
        def sent(t, _):
            @pl.when(t != p)
            def _():
                await_bytes(qs.at[pl.ds(pl.multiple_of(48 * t, 8), 48)], s_o.at[t])

            return 0

        lax.fori_loop(0, 8, sent, 0)

    await_bytes(xin, s_out.at[0])


def call(lower, upper, fermi, height, x, v):
    smem = pl.BlockSpec(memory_space=pltpu.SMEM)
    vmem = pl.BlockSpec(memory_space=pltpu.VMEM)
    hbm = pl.BlockSpec(memory_space=pl.ANY)
    sem = pltpu.SemaphoreType.DMA
    consts = tables()

    def buf(*shape):
        return pltpu.VMEM(shape, F32)

    return pl.pallas_call(
        kernel,
        out_shape=(
            jax.ShapeDtypeStruct((6, 144, 128), F32),
            jax.ShapeDtypeStruct((2,), F32),
            jax.ShapeDtypeStruct((1,), F32),
        ),
        in_specs=[smem] * 3 + [vmem] + [hbm] * 8,
        out_specs=(hbm, smem, smem),
        scratch_shapes=[
            buf(6, 144, 128),
            buf(2, 96, 128),
            *[pltpu.VMEM(t.shape, BF16) for t in consts],
            buf(6, 64, 128),
            buf(8, 64, 128),
            buf(6, 96, 96),
            buf(8, 64, 128),
            buf(8, 64, 128),
            buf(8, 64, 128),
            buf(8, 64, 128),
            buf(8, 64, 128),
            buf(2, 384, 128),
            buf(2, 7, 24, 128),
            buf(2, 7, 24, 128),
            buf(2, 384, 128),
            buf(2, 384, 128),
            pltpu.VMEM((32, 3072), BF16),
            pltpu.VMEM((32, 3072), BF16),
            buf(4, 128),
            buf(8, 4, 128),
            buf(4, 128),
            buf(17, 4, 128),
            buf(1, 128),
            buf(8, 1, 128),
            buf(1, 128),
            buf(17, 1, 128),
            buf(384, 128),
            buf(7, 48, 128),
            sem((1,)),
            sem((1,)),
            sem((6,)),
            sem((6,)),
            sem((8,)),
            sem((8,)),
            sem((2,)),
            sem((2, 16)),
            sem((2, 7)),
            sem((2, 7)),
            sem((2, 16)),
            sem((2, 56)),
            sem((2, 3, 16)),
            sem((2, 8)),
            sem((2, 8)),
            sem((2, 32)),
            sem((2, 17)),
            sem((8,)),
            sem((7,)),
            pltpu.SemaphoreType.REGULAR,
        ],
        compiler_params=pltpu.CompilerParams(
            has_side_effects=True, collective_id=0, vmem_limit_bytes=60 * 2**20
        ),
    )(lower, upper, fermi, height, x, v, *[jnp.asarray(t) for t in consts])


def local(start_bands, potential, half_height, lower_bound, upper_bound, fermi_level):
    x = start_bands.reshape(2, 2, 3, 72, 128).transpose(0, 2, 3, 1, 4).reshape(6, 144, 128)
    v = potential.transpose(2, 0, 1)
    out, energies, band_energy = call(lower_bound, upper_bound, fermi_level, half_height, x, v)
    out = out.reshape(2, 3, 72, 2, 128).transpose(0, 3, 1, 2, 4).reshape(2, 2, 3, NG * NG)
    return out, energies, band_energy


def solution(mesh):
    placed = (P(None, "band", "fft", None), P(None, None, "fft"), P("fft", None), P(), P(), P())
    return jax.shard_map(
        local,
        mesh=mesh,
        in_specs=placed,
        out_specs=(P(None, "band", "fft", None), P("band"), P()),
        check_vma=False,
    )
```

time: 131 us -> 121 us (0.924)
  Pallas kernels: 119 us -> 115 us
  local copies, waits for them, and re-layouts: 5.69 us -> 2.32 us
  other arithmetic: 2.23 us -> 0 us
    pallas_call x1, Pallas kernels: 119 us -> 115 us  [call(): pl.pallas_call(kernel, out_shape=(jax.ShapeDtypeStruct((6, 144, 128), F32...]
    reshape x2 -> x0, local copies, waits for them, and re-layouts: 1.8 us -> none  [the longest x1 1.37 us: local(): bands = unboxed(unboxed(q, 3), 4).reshape(2, 2, 3, NG * NG)]
    concatenate x6 -> x0, other arithmetic: 1.6 us -> none  [the longest x3 1.09 us: boxed(): return jnp.concatenate([low, x[tuple(index)]], axis=axis)]
    unnamed x10 -> x4, local copies, waits for them, and re-layouts: 0.94 us -> 2.32 us
where the time goes in v1:
time: 121 us
  Pallas kernels  115 us (95%)
  between operations  4.35 us (4%)
  local copies, waits for them, and re-layouts  2.32 us (2%)
    pallas_call x1, Pallas kernels, call(): pl.pallas_call(kernel, out_shape=(jax.ShapeDtypeStruct((6, 144, 128), F32...  115 us

profile of v1, /device:TPU:1, one launch (start us, length us, event | category | flops | bytes accessed | tf_op | source)
XLA Modules:
  0.0 121.3 jit_solution(13425493383736445247)
XLA Ops:
  2.6 114.6 %shard_map.139 = (f32[6,144,128]{2,1,0:T(8,128)}, f32[2]{0:T(128)}, f32[1]{0:T(128)}) custom-call(f32[1]{0:T(128)S(6)} %copy.20.lower_ref, f32[1]{0:T(128)S(6)} %copy.21.upper_ref, f32[1]{0:T(128)S(6)} %copy.22.fermi_ref, s32[3,96]{1,0:T(4,128)} %height_ref.1, f32[6,144,128]{2,1,0:T(8,128)} %bitcast.11, f32[3,96,96]{2,1,0:T(8,128)} %bitcast.13, ...), custom_call_target="tpu_custom_call" | custom-call | tf_op jit(solution)/shard_map/pallas_call | solution.py:791
  117.2 0.0 copy-start
  117.2 1.8 %copy.23 = f32[2,2,3,9216]{3,1,2,0:T(2,128)} copy(f32[2,2,3,9216]{3,1,2,0:T(2,128)} %bitcast.12) | data formatting | bytes 884736
  119.0 0.0 copy-done
  119.0 0.5 copy.24
Async XLA Ops:
  117.2 1.8 %copy-start = (f32[2]{0:T(128)S(1)}, f32[2]{0:T(128)}, u32[]{:S(2)}) copy-start(f32[2]{0:T(128)} %get-tuple-element.13) | copy-start | bytes 28

commit v2 on v1

v2 whole, which is shorter than its diff:
```python
import math

import jax
import jax.numpy as jnp
import ml_dtypes
import numpy as np
from jax import lax
from jax.experimental import pallas as pl
from jax.experimental.pallas import tpu as pltpu
from jax.sharding import PartitionSpec as P

NG = 96
CELLS = float(NG**3)
BOX = 49
KIN = 12.0 / 24**2
TEMPER = 0.5
BANDS = 16
ACTIVE = (*range(9), *range(24, 32))
MEMBERS = 16
HOLDERS = 7
ZP = 3
F32, BF16 = jnp.float32, jnp.bfloat16
MESH = pl.DeviceIdType.MESH


def box_frequency():
    r = np.arange(BOX)
    return np.where(r <= 24, r, r - BOX)


def halves(table):
    table = table.astype(np.float32)
    high = table.astype(ml_dtypes.bfloat16)
    low = (table - high.astype(np.float32)).astype(ml_dtypes.bfloat16)
    return high, low


def tables():
    freq = box_frequency()
    angle = 2.0 * math.pi / NG * ((np.arange(NG)[:, None] * freq[None, :]) % NG)
    cosine, sine = np.cos(angle), np.sin(angle)
    ahead = np.zeros((192, 64))
    ahead[:96, :BOX], ahead[96:, :BOX] = cosine, sine
    back = np.zeros((128, 96))
    back[:BOX], back[64 : 64 + BOX] = cosine.T, sine.T
    lanes = np.zeros((128, 256))
    lanes[:BOX, :96], lanes[:BOX, 128:224] = cosine.T, sine.T
    lanes[64 : 64 + BOX, :96], lanes[64 : 64 + BOX, 128:224] = -sine.T, cosine.T
    lanes_back = lanes.T.copy()
    plane = np.arange(NG).reshape(MEMBERS, 2, ZP)

    def left(t):
        high, low = halves(t)
        return np.concatenate([high, high, low], axis=1)

    def right(t):
        high, low = halves(t)
        return np.concatenate([high, high, low], axis=0)

    z_ahead = [np.concatenate([ahead[plane[:, h].ravel()], ahead[96 + plane[:, h].ravel()]]) for h in range(2)]
    z_back = [back[:, plane[:, h].ravel()] for h in range(2)]
    return (
        np.stack([left(t) for t in z_ahead]),
        left(ahead),
        np.stack([left(t) for t in z_back]),
        left(back),
        right(lanes),
        right(lanes_back),
    )


def split(x):
    high = x.astype(BF16)
    return high, (x - high.astype(F32)).astype(BF16)


def pieces(x, axis):
    high, low = split(x)
    return jnp.concatenate([high, low, high], axis=axis)


def dot(a, b):
    return jnp.dot(a, b, preferred_element_type=F32)


def dot_t(a, b):
    return lax.dot_general(a, b, (((1,), (1,)), ((), ())), preferred_element_type=F32)


def kernel(
    lower_ref,
    upper_ref,
    fermi_ref,
    height_hbm,
    x_hbm,
    v_hbm,
    tz_hbm,
    tx_hbm,
    tzb_hbm,
    txb_hbm,
    ty_hbm,
    tyb_hbm,
    out_hbm,
    energy_ref,
    band_energy_ref,
    xin,
    grid,
    height_ref,
    vin,
    vp,
    vb,
    vfull,
    acc,
    tz,
    tx,
    tzb,
    txb,
    ty,
    tyb,
    xt,
    x0,
    cur,
    prev,
    hy,
    inside,
    kin,
    sbuf,
    rbuf,
    bbuf,
    kbuf,
    gy,
    bh,
    bl,
    part,
    col,
    csum,
    full,
    epart,
    ecol,
    ecsum,
    efull,
    qs,
    ob,
    s_in,
    s_out,
    s_t,
    s_init,
    r_init,
    s_v,
    r_v,
    s_f,
    r_f,
    s_b,
    r_b,
    s_g,
    r_g,
    s_c,
    r_c,
    s_p,
    r_p,
    s_o,
    r_o,
    planes_in,
):
    p = lax.axis_index("band")
    i = lax.axis_index("fft")

    def quot(a, n):
        return a // n if isinstance(a, int) else lax.div(a, jnp.int32(n))

    def mod(a, n):
        return a % n if isinstance(a, int) else lax.rem(a, jnp.int32(n))

    def both(a, b):
        return jnp.logical_and(a, b)

    y, core = quot(p, 2), mod(p, 2)
    y2, yl = quot(y, 2), mod(y, 2)
    gx, gzz = quot(i, 8), mod(i, 8)
    x2, xl = quot(gx, 2), mod(gx, 2)
    gz, zl = quot(gzz, 2), mod(gzz, 2)
    band = 8 * y2 + 4 * x2 + gz
    xr = 2 * yl + mod(xl + yl, 2)
    zr = 2 * core + mod(zl + core, 2)
    place = 4 * xr + zr
    me = 4 * mod(xr + 2 * x2, 4) + mod(zr + gz, 4)
    chip = 2 * xr + zr - 2
    is_k = both(core == 1, chip < HOLDERS)
    active = jnp.logical_or(i <= 8, i >= 24)
    lone = i == 8
    summing = both(active, p < 7)

    def dev(pp, ii):
        return {"band": pp, "fft": ii}

    def at_place(yy, xx, zz, xr_, zr_):
        c = quot(zr_, 2)
        return dev(
            4 * yy + 2 * quot(xr_, 2) + c,
            16 * xx + 8 * mod(quot(xr_ + 1, 2), 2) + 2 * zz + mod(quot(zr_ + 1, 2), 2),
        )

    def holder(b, s):
        return at_place(quot(b, 8), mod(quot(b, 4), 2), mod(b, 4), quot(s, 2), 2 + mod(s, 2))

    def mine_at(n):
        return at_place(y2, x2, gz, n // 4, n % 4)

    def slab_of(n):
        return 4 * mod(n // 4 + 2 * x2, 4) + mod(n % 4 + gz, 4)

    def is_me(where):
        return both(where["band"] == p, where["fft"] == i)

    def remote(src, dst, ss, rs, where):
        return pltpu.make_async_remote_copy(
            src_ref=src, dst_ref=dst, send_sem=ss, recv_sem=rs, device_id=where, device_id_type=MESH
        )

    def await_bytes(ref, sem):
        pltpu.make_async_copy(ref, ref, sem).wait()

    for src, dst, n in ((x_hbm, xin, 0), (v_hbm, vin, 1), (height_hbm, height_ref, 2)):
        pltpu.make_async_copy(src, dst, s_in.at[n]).start()
    for n, (src, dst) in enumerate(
        ((tz_hbm, tz), (tx_hbm, tx), (tzb_hbm, tzb), (txb_hbm, txb), (ty_hbm, ty), (tyb_hbm, tyb))
    ):
        pltpu.make_async_copy(src, dst, s_t.at[n]).start()

    barrier = pltpu.get_barrier_semaphore()

    def tell(where):
        pl.semaphore_signal(barrier, inc=1, device_id=where, device_id_type=MESH)

    def kx_of_slot(a):
        q = 8 * chip + a
        return q < BOX, jnp.where(q <= 24, q, q + 47)

    @pl.when(is_k)
    def _():
        for a in range(8):
            held, kx = kx_of_slot(a)
            native = dev(quot(band, 2), quot(kx, 3))

            @pl.when(both(held, jnp.logical_not(is_me(native))))
            def _():
                tell(native)

    for h in range(2):
        source = dev(2 * y + quot(gz, 2), 2 * me + h)

        @pl.when(jnp.logical_not(is_me(source)))
        def _():
            tell(source)

    for n in range(MEMBERS):

        @pl.when(place != n)
        def _():
            tell(mine_at(n))

    def counterpart(n):
        return at_place(
            mod(y2 + n // 8, 2), mod(x2 + (n // 4) % 2, 2), mod(gz + n % 4, 4), xr, zr
        )

    for n in range(1, 16):
        tell(counterpart(n))

    def start_of(k):
        j, jj = k // 3, k % 3
        kx = 3 * i + jj
        valid = jnp.logical_or(kx <= 24, kx >= 72)
        q = jnp.where(kx <= 24, kx, kx - 47)
        s = jnp.minimum(jnp.maximum(quot(q, 8), 0), HOLDERS - 1)
        return valid, mod(q, 8), holder(2 * p + j, s)

    def v_target(n):
        xx = mod(quot(gx, 2) + yl, 2)
        zz = 2 * core + n
        return at_place(y2, xx, zz, mod(gx + 2 * xx, 4), mod(quot(gzz, 2) - zz + 4, 4))

    expected = jnp.int32(30)
    for k in range(6):
        valid, _, target = start_of(k)
        expected = expected + both(valid, jnp.logical_not(is_me(target))).astype(jnp.int32)
    for n in range(2):
        expected = expected + jnp.logical_not(is_me(v_target(n))).astype(jnp.int32)

    lane = lax.broadcasted_iota(jnp.int32, (1, 128), 1)
    sign = jnp.where(lane < 64, -1.0, 1.0).astype(F32)

    def swap(x):
        return pltpu.roll(x, 64, 1)

    def boxed_lanes(x):
        return jnp.where(lane < 25, x, jnp.where(lane < BOX, pltpu.roll(x, 128 - 47, 1), 0.0))

    def unpack(t0, t1, t2):
        return (
            t0,
            jnp.where(lane < 32, pltpu.roll(t0, 32, 1), pltpu.roll(t1, 32, 1)),
            jnp.where(lane < 64, pltpu.roll(t1, 64, 1), pltpu.roll(t2, 64, 1)),
            pltpu.roll(t2, 96, 1),
        )

    def pack(o0, o1, o2, o3):
        return (
            jnp.where(lane < 96, o0, pltpu.roll(o1, 96, 1)),
            jnp.where(lane < 64, pltpu.roll(o1, 96, 1), pltpu.roll(o2, 64, 1)),
            jnp.where(lane < 32, pltpu.roll(o2, 64, 1), pltpu.roll(o3, 32, 1)),
        )

    await_bytes(xin, s_in.at[0])
    await_bytes(height_ref, s_in.at[2])
    for k in range(6):
        j, jj = k // 3, k % 3
        for c in range(2):
            quarter = unpack(*(xin[3 * c + jj, pl.ds(2 * t + j, 24, stride=6), :] for t in range(3)))
            for r in range(4):
                grid[c, pl.ds(r, 24, stride=4), :] = boxed_lanes(quarter[r])
        pad = jnp.zeros((15, 128), F32)
        rows = jnp.concatenate([grid[0, 0:25], grid[0, 72:96], pad, grid[1, 0:25], grid[1, 72:96], pad], axis=0)
        xt[k] = rows.T[:56]
    for jj in range(3):
        h = height_ref[jj : jj + 1, :].astype(F32)
        h = boxed_lanes(jnp.concatenate([h, jnp.zeros((1, 32), F32)], axis=1))
        h = jnp.where(lane < BOX, h, -1.0)
        h = jnp.where(lane < 64, h, pltpu.roll(h, 64, 1))
        for j in range(2):
            xt[3 * j + jj, BOX : BOX + 1, :] = h
    await_bytes(vin, s_in.at[1])
    for z in range(3):
        grid[0] = jnp.concatenate([vin[z], jnp.zeros((96, 32), F32)], axis=1)
        thirds = pack(*(grid[0, pl.ds(r, 24, stride=4), :] for r in range(4)))
        for t in range(3):
            vp[z, 24 * t : 24 * t + 24, :] = thirds[t]

    pl.semaphore_wait(barrier, expected)

    for k in range(6):
        valid, slot, target = start_of(k)

        @pl.when(both(valid, is_me(target)))
        def _():
            pltpu.make_async_copy(xt.at[k], x0.at[slot], r_init.at[slot]).start()

        @pl.when(both(valid, jnp.logical_not(is_me(target))))
        def _():
            remote(xt.at[k], x0.at[slot], s_init.at[k], r_init.at[slot], target).start()

    for n in range(2):
        target = v_target(n)
        home = vb.at[pl.ds(3 * mod(i, 2), 3)]

        @pl.when(is_me(target))
        def _():
            pltpu.make_async_copy(vp, home, r_v.at[mod(i, 2)]).start()

        @pl.when(jnp.logical_not(is_me(target)))
        def _():
            remote(vp, home, s_v.at[n], r_v.at[mod(i, 2)], target).start()

    for n in range(1, 16):
        pl.semaphore_signal(planes_in, inc=1, device_id=counterpart(n), device_id_type=MESH)

    for n, dst in enumerate((tz, tx, tzb, txb, ty, tyb)):
        await_bytes(dst, s_t.at[n])

    @pl.when(is_k)
    def _():
        row = lax.broadcasted_iota(jnp.int32, (64, 128), 0)
        col_ = lax.broadcasted_iota(jnp.int32, (64, 128), 1) % 64
        fz = jnp.where(row <= 24, row, row - BOX)
        fy = jnp.where(col_ <= 24, col_, col_ - BOX)
        in_box = jnp.logical_and(row < BOX, col_ < BOX)
        yz = (fz * fz + fy * fy).astype(F32)
        absz = jnp.abs(fz).astype(F32)

        def plane(a, _):
            q = 8 * chip + a

            @pl.when(q < BOX)
            def _():
                await_bytes(x0.at[a], r_init.at[a])
                fx = jnp.where(q <= 24, q, q - BOX)
                data = x0[a]
                data = jnp.concatenate([data, jnp.zeros((8, 128), F32)], axis=0)
                keep = both(in_box, absz <= data[BOX : BOX + 1])
                cur[a] = jnp.where(keep, data, 0.0)
                inside[a] = jnp.where(keep, 1.0 / CELLS, 0.0)
                kin[a] = jnp.where(keep, KIN * (yz + (fx * fx).astype(F32)), 0.0)

            @pl.when(q >= BOX)
            def _():
                zero = jnp.zeros((64, 128), F32)
                cur[a] = zero
                inside[a] = zero
                kin[a] = zero

            prev[a] = jnp.zeros((64, 128), F32)
            return 0

        lax.fori_loop(0, 8, plane, 0)

    def message(m):
        return pl.ds(pl.multiple_of(24 * m, 8), 24)

    def forward():
        @pl.when(is_k)
        def _():
            x = pieces(jnp.concatenate([cur[a] for a in range(8)], axis=1), 0)
            for h in range(2):
                out = dot(tz[h], x)
                for a in range(8):
                    c, s = out[:48, 128 * a : 128 * a + 128], out[48:, 128 * a : 128 * a + 128]
                    sbuf[h, pl.ds(a, 48, stride=8), :] = c + sign * swap(s)

                for n in range(MEMBERS):
                    src = sbuf.at[h, message(slab_of(n))]
                    home = rbuf.at[h, chip]

                    @pl.when(place == n)
                    def _():
                        pltpu.make_async_copy(src, home, r_f.at[h]).start()

                    @pl.when(place != n)
                    def _():
                        remote(src, home, s_f.at[h], r_f.at[h], mine_at(n)).start()

    def middle(first):
        zero8 = jnp.zeros((8, 128), F32)
        for h in range(2):
            await_bytes(rbuf.at[h], r_f.at[h])
            d = jnp.concatenate(
                [
                    jnp.concatenate(
                        [rbuf[h, s, 8 * z : 8 * z + 8, :] for s in range(HOLDERS)] + [zero8], axis=0
                    )
                    for z in range(ZP)
                ],
                axis=1,
            )
            out = dot(tx[...], pieces(d, 0))
            rows = jnp.concatenate(
                [
                    out[:96, 128 * z : 128 * z + 128] + sign * swap(out[96:, 128 * z : 128 * z + 128])
                    for z in range(ZP)
                ],
                axis=0,
            )
            psi = dot(pieces(rows, 1), ty[...])

            @pl.when(first)
            def _():
                await_bytes(vb.at[pl.ds(3 * h, 3)], r_v.at[h])
                for z in range(3 * h, 3 * h + 3):
                    quarter = unpack(*(vb[z, 24 * t : 24 * t + 24, :] for t in range(3)))
                    for r in range(4):
                        vfull[z, pl.ds(r, 24, stride=4), :] = jnp.where(lane < NG, quarter[r], 0.0)

            v = jnp.concatenate([vfull[3 * h + z] for z in range(ZP)], axis=0)
            psi = psi * jnp.concatenate([v, v], axis=1)
            rows = dot(pieces(psi, 1), tyb[...])
            d = jnp.concatenate([rows[96 * z : 96 * z + 96] for z in range(ZP)], axis=1)
            out = dot(txb[...], pieces(d, 0))
            for z in range(ZP):
                o = out[:64, 128 * z : 128 * z + 128] - sign * swap(out[64:, 128 * z : 128 * z + 128])
                for s in range(HOLDERS):
                    bbuf[h, s, 8 * z : 8 * z + 8, :] = o[8 * s : 8 * s + 8]

            for s in range(HOLDERS):
                home = kbuf.at[h, message(me)]
                mine = both(is_k, chip == s)

                @pl.when(mine)
                def _():
                    pltpu.make_async_copy(bbuf.at[h, s], home, r_b.at[h]).start()

                @pl.when(jnp.logical_not(mine))
                def _():
                    remote(bbuf.at[h, s], home, s_b.at[h], r_b.at[h], mine_at(4 * (s // 2) + 2 + s % 2)).start()

    def backward(finish):
        @pl.when(is_k)
        def _():
            for h in range(2):
                await_bytes(kbuf.at[h], r_b.at[h])
                d = jnp.concatenate([kbuf[h, pl.ds(a, 48, stride=8), :] for a in range(8)], axis=1)
                term = dot(tzb[h], pieces(d, 0))
                acc[...] = acc[...] + term if h else term
            for a in range(8):
                f = acc[:64, 128 * a : 128 * a + 128] - sign * swap(acc[64:, 128 * a : 128 * a + 128])
                finish(a, kin[a] * cur[a] + inside[a] * f)
            for h in range(2):
                await_bytes(sbuf.at[h, pl.ds(0, 24 * (MEMBERS - 1))], s_f.at[h])
                await_bytes(bbuf.at[h, pl.ds(0, HOLDERS - 1)], s_b.at[h])

        @pl.when(jnp.logical_not(is_k))
        def _():
            for h in range(2):
                await_bytes(bbuf.at[h], s_b.at[h])

    center = 0.5 * (upper_ref[0] + lower_ref[0])
    half_width = 0.5 * (upper_ref[0] - lower_ref[0])

    def step(k, _):
        forward()
        middle(k == 0)
        alpha = jnp.where(k == 0, 1.0, 2.0).astype(F32)
        beta = jnp.where(k == 0, 0.0, 1.0).astype(F32)

        def finish(a, h):
            old = cur[a]
            new = alpha * (h - center * old) / half_width - beta * prev[a]
            prev[a] = old
            cur[a] = new

        backward(finish)
        return 0

    lax.fori_loop(0, 3, step, 0)

    def for_rows(do):
        @pl.when(is_k)
        def _():
            for a in range(8):
                held, kx = kx_of_slot(a)
                home, jj = quot(kx, 3), mod(kx, 3)

                @pl.when(held)
                def _():
                    for t in range(7):
                        target = dev(t, home)
                        do(a, t, jj, target)

    def scatter(src, w):
        def one(a, t, jj, target):
            dst = gy.at[w, pl.ds(pl.multiple_of(128 * jj + 8 * band, 8), 8)]
            row = src.at[a, pl.ds(8 * t, 8)]

            @pl.when(is_me(target))
            def _():
                pltpu.make_async_copy(row, dst, r_g.at[w]).start()

            @pl.when(jnp.logical_not(is_me(target)))
            def _():
                remote(row, dst, s_g.at[w, 7 * a + t], r_g.at[w], target).start()

        for_rows(one)

    def scattered(src, w):
        def one(a, t, jj, target):
            @pl.when(jnp.logical_not(is_me(target)))
            def _():
                await_bytes(src.at[a, pl.ds(8 * t, 8)], s_g.at[w, 7 * a + t])

        for_rows(one)

    def all_rows(w):
        @pl.when(lone)
        def _():
            await_bytes(gy.at[w, pl.ds(0, 128)], r_g.at[w])

        @pl.when(jnp.logical_not(lone))
        def _():
            await_bytes(gy.at[w], r_g.at[w])

        rows = []
        for jj in range(3):
            for r in range(8):
                x = gy[w, pl.ds(128 * jj + r, BANDS, stride=8), :]
                rows.append(jnp.where(lone, 0.0, x) if jj else x)
        a = jnp.concatenate(rows, axis=1)
        b = jnp.concatenate([-sign * swap(x) for x in rows], axis=1)
        return jnp.concatenate([a, b], axis=0)

    my_slot = jnp.minimum(jnp.where(i <= 8, i, jnp.maximum(i - 15, 0)), 16)

    def column_send(w, mine, theirs):
        for t in range(8):

            @pl.when(p != t)
            def _():
                remote(mine, theirs.at[p], s_c.at[w], r_c.at[w], dev(t, i)).start()

    def column_sum(w, theirs):
        @pl.when(p < 7)
        def _():
            await_bytes(theirs.at[pl.ds(0, 6)], r_c.at[w])

        @pl.when(p == 7)
        def _():
            await_bytes(theirs.at[pl.ds(0, 7)], r_c.at[w])

        total = theirs[0]
        for t in range(1, 7):
            total = total + theirs[t]
        return total

    def plane_send(w, mine, theirs, targets):
        for ii in targets:

            @pl.when(i != ii)
            def _():
                remote(mine, theirs.at[my_slot], s_p.at[w], r_p.at[w], dev(p, ii)).start()

    def plane_sum(w, theirs):
        @pl.when(active)
        def _():
            await_bytes(theirs.at[pl.ds(0, 16)], r_p.at[w])

        @pl.when(jnp.logical_not(active))
        def _():
            await_bytes(theirs.at[pl.ds(0, 17)], r_p.at[w])

        total = theirs[0]
        for n in range(1, 17):
            total = total + theirs[n]
        return total

    lane2 = lax.broadcasted_iota(jnp.int32, (16, 128), 1)

    def inverse_rows(g):
        row = lax.broadcasted_iota(jnp.int32, (32, 128), 0)
        ln = lax.broadcasted_iota(jnp.int32, (32, 128), 1)
        top = jnp.where(lane2 < 16, g, -g)
        bottom = jnp.where(lane2 < 16, pltpu.roll(g, 112, 1), pltpu.roll(g, 16, 1))
        m = jnp.where(ln < 32, jnp.concatenate([top, bottom], 0), 0.0)
        m = m + jnp.where(ln == row + 32, 1.0, 0.0)
        for j in range(32):
            pivot = m[j : j + 1, :]
            factor = m[:, j : j + 1] * (1.0 / pivot[:, j : j + 1])
            m = m - jnp.where(row > j, factor, 0.0) * pivot
        diag = jnp.sum(jnp.where(ln == row, m, 0.0), axis=1, keepdims=True)
        u = m[:16] / jnp.sqrt(diag[:16])
        return jnp.where(lane2 < 32, pltpu.roll(u, 96, 1), 0.0)

    pl.semaphore_wait(planes_in, 15)
    scatter(cur, 0)
    forward()
    middle(False)

    @pl.when(summing)
    def _():
        high, low = split(all_rows(0))
        bh[...] = high
        bl[...] = low
        g = (dot_t(bh[:BANDS], high) + dot_t(bh[:BANDS], low) + dot_t(bl[:BANDS], high)) * (1.0 / CELLS)
        g = jnp.concatenate([g, jnp.zeros((BANDS, 96), F32)], axis=1)
        packed = g[0:4]
        for n in range(1, 4):
            packed = packed + pltpu.roll(g[4 * n : 4 * n + 4], 32 * n, 1)
        part[...] = packed
        col[p] = packed
        column_send(0, part, col)

    @pl.when(active)
    def _():
        total = column_sum(0, col)
        csum[...] = total
        full[my_slot] = total
        plane_send(0, csum, full, ACTIVE)

    def keep(a, h):
        hy[a] = h

    backward(keep)
    scatter(hy, 1)

    @pl.when(active)
    def _():
        total = plane_sum(0, full)

        @pl.when(p < 7)
        def _():
            g = jnp.concatenate([total] + [pltpu.roll(total, 128 - 32 * n, 1) for n in range(1, 4)], axis=0)
            u = inverse_rows(jnp.where(lane2 < 32, g, 0.0))
            w_high, w_low = split(jnp.where(lane2 < 16, u, -u)[:, :32])

            def rotated(high, low):
                return dot(w_high, high) + dot(w_high, low) + dot(w_low, high)

            q = rotated(bh[...], bl[...])
            for n in range(24):
                qs[pl.ds(n, BANDS, stride=24), :] = q[:, 128 * n : 128 * n + 128]

            for t in range(8):
                src = qs.at[pl.ds(48 * t, 48)]

                @pl.when(p == t)
                def _():
                    pltpu.make_async_copy(src, ob.at[p], r_o.at[0]).start()

                @pl.when(p != t)
                def _():
                    remote(src, ob.at[p], s_o.at[0], r_o.at[0], dev(t, i)).start()

            hq = rotated(*split(all_rows(1)))
            e = q[:, :128] * hq[:, :128]
            for n in range(1, 24):
                e = e + q[:, 128 * n : 128 * n + 128] * hq[:, 128 * n : 128 * n + 128]
            e = jnp.sum(e, axis=1, keepdims=True) * (1.0 / CELLS)
            row = lax.broadcasted_iota(jnp.int32, (16, 128), 0)
            e = jnp.sum(jnp.where(lane2 == row, e, 0.0), axis=0, keepdims=True)
            epart[...] = e
            ecol[p] = e
            column_send(1, epart, ecol)

        total = column_sum(1, ecol)
        ecsum[...] = total
        efull[my_slot] = total
        plane_send(1, ecsum, efull, range(32))

        await_bytes(ob, r_o.at[0])
        zero = jnp.zeros((72, 128), F32)
        low_lanes, high_lanes = lane < 25, jnp.logical_and(lane >= 72, lane < 96)
        for k in range(6):
            j, jj = k // 3, k % 3
            rows = jnp.concatenate([ob[t, 8 * k : 8 * k + 8, :] for t in range(7)] + [zero], axis=0)
            if jj:
                rows = jnp.where(lone, 0.0, rows)
            rows = rows.T
            rows = jnp.where(low_lanes, rows, jnp.where(high_lanes, pltpu.roll(rows, 47, 1), 0.0))
            for c in range(2):
                grid[c, 0:25] = rows[64 * c : 64 * c + 25]
                grid[c, 25:72] = jnp.zeros((47, 128), F32)
                grid[c, 72:96] = rows[64 * c + 25 : 64 * c + BOX]
                thirds = pack(*(grid[c, pl.ds(r, 24, stride=4), :] for r in range(4)))
                for t in range(3):
                    xin[3 * c + jj, pl.ds(2 * t + j, 24, stride=6), :] = thirds[t]

    @pl.when(jnp.logical_not(active))
    def _():
        xin[...] = jnp.zeros((6, 144, 128), F32)

    pltpu.make_async_copy(xin, out_hbm, s_out.at[0]).start()

    for k in range(6):
        valid, _, target = start_of(k)

        @pl.when(both(valid, jnp.logical_not(is_me(target))))
        def _():
            await_bytes(xt.at[k], s_init.at[k])

    for n in range(2):

        @pl.when(jnp.logical_not(is_me(v_target(n))))
        def _():
            await_bytes(vp, s_v.at[n])

    scattered(cur, 0)
    scattered(hy, 1)

    @pl.when(summing)
    def _():
        await_bytes(col.at[pl.ds(0, 7)], s_c.at[0])
        await_bytes(ecol.at[pl.ds(0, 7)], s_c.at[1])
        await_bytes(qs.at[pl.ds(0, 48 * 7)], s_o.at[0])

    @pl.when(active)
    def _():
        await_bytes(full.at[pl.ds(0, 16)], s_p.at[0])
        await_bytes(efull.at[pl.ds(0, 31)], s_p.at[1])

    await_bytes(xin, s_out.at[0])

    e = plane_sum(1, efull)
    for j in range(2):
        energy_ref[j] = jnp.sum(jnp.where(lane == 2 * p + j, e, 0.0))
    weights = jax.nn.sigmoid((fermi_ref[0] - e) / TEMPER)
    band_energy_ref[0] = jnp.sum(jnp.where(lane < BANDS, weights * e, 0.0)) / float(BANDS)


def call(lower, upper, fermi, height, x, v):
    smem = pl.BlockSpec(memory_space=pltpu.SMEM)
    hbm = pl.BlockSpec(memory_space=pl.ANY)
    sem = pltpu.SemaphoreType.DMA
    consts = tables()

    def buf(*shape):
        return pltpu.VMEM(shape, F32)

    return pl.pallas_call(
        kernel,
        out_shape=(
            jax.ShapeDtypeStruct((6, 144, 128), F32),
            jax.ShapeDtypeStruct((2,), F32),
            jax.ShapeDtypeStruct((1,), F32),
        ),
        in_specs=[smem] * 3 + [hbm] * 9,
        out_specs=(hbm, smem, smem),
        scratch_shapes=[
            buf(6, 144, 128),
            buf(2, 96, 128),
            pltpu.VMEM((3, 96), jnp.int32),
            buf(3, 96, 96),
            buf(3, 72, 128),
            buf(6, 72, 128),
            buf(6, 96, 128),
            buf(128, 1024),
            *[pltpu.VMEM(t.shape, BF16) for t in consts],
            buf(6, 56, 128),
            buf(8, 56, 128),
            buf(8, 64, 128),
            buf(8, 64, 128),
            buf(8, 64, 128),
            buf(8, 64, 128),
            buf(8, 64, 128),
            buf(2, 384, 128),
            buf(2, 7, 24, 128),
            buf(2, 7, 24, 128),
            buf(2, 384, 128),
            buf(2, 384, 128),
            pltpu.VMEM((32, 3072), BF16),
            pltpu.VMEM((32, 3072), BF16),
            buf(4, 128),
            buf(8, 4, 128),
            buf(4, 128),
            buf(17, 4, 128),
            buf(1, 128),
            buf(8, 1, 128),
            buf(1, 128),
            buf(32, 1, 128),
            buf(384, 128),
            buf(7, 48, 128),
            sem((3,)),
            sem((1,)),
            sem((6,)),
            sem((6,)),
            sem((8,)),
            sem((2,)),
            sem((2,)),
            sem((2,)),
            sem((2,)),
            sem((2,)),
            sem((2,)),
            sem((2, 56)),
            sem((2,)),
            sem((2,)),
            sem((2,)),
            sem((2,)),
            sem((2,)),
            sem((1,)),
            sem((1,)),
            pltpu.SemaphoreType.REGULAR,
        ],
        compiler_params=pltpu.CompilerParams(
            has_side_effects=True, collective_id=0, vmem_limit_bytes=60 * 2**20
        ),
    )(lower, upper, fermi, height, x, v, *[jnp.asarray(t) for t in consts])


def local(start_bands, potential, half_height, lower_bound, upper_bound, fermi_level):
    x = start_bands.reshape(2, 2, 3, 72, 128).transpose(0, 2, 3, 1, 4).reshape(6, 144, 128)
    v = potential.transpose(2, 0, 1)
    out, energies, band_energy = call(lower_bound, upper_bound, fermi_level, half_height, x, v)
    out = out.reshape(2, 3, 72, 2, 128).transpose(0, 3, 1, 2, 4).reshape(2, 2, 3, NG * NG)
    return out, energies, band_energy


def solution(mesh):
    placed = (P(None, "band", "fft", None), P(None, None, "fft"), P("fft", None), P(), P(), P())
    return jax.shard_map(
        local,
        mesh=mesh,
        in_specs=placed,
        out_specs=(P(None, "band", "fft", None), P("band"), P()),
        check_vma=False,
    )
```

time: 121 us -> 98 us (0.81)
  Pallas kernels: 115 us -> 91.2 us
    pallas_call x1, Pallas kernels: 115 us -> 91.2 us  [call(): pl.pallas_call(kernel, out_shape=(jax.ShapeDtypeStruct((6, 144, 128), F32...]
where the time goes in v2:
time: 98 us; the launch traced here: 97.8 us
  Pallas kernels  91.2 us (93%)
  between operations  4.35 us (4%)
  local copies, waits for them, and re-layouts  2.32 us (2%)
    pallas_call x1, Pallas kernels, call(): pl.pallas_call(kernel, out_shape=(jax.ShapeDtypeStruct((6, 144, 128), F32...  91.2 us
    unnamed x4, local copies, waits for them, and re-layouts  2.32 us

profile of v2, /device:TPU:1, one launch (start us, length us, event | category | flops | bytes accessed | tf_op | source)
XLA Modules:
  0.0 97.8 jit_solution(377911933689806978)
XLA Ops:
  2.6 91.2 %shard_map.139 = (f32[6,144,128]{2,1,0:T(8,128)}, f32[2]{0:T(128)}, f32[1]{0:T(128)}) custom-call(f32[1]{0:T(128)S(6)} %copy.20.lower_ref, f32[1]{0:T(128)S(6)} %copy.21.upper_ref, f32[1]{0:T(128)S(6)} %copy.22.fermi_ref, s32[3,96]{1,0:T(4,128)} %height_hbm.1, f32[6,144,128]{2,1,0:T(8,128)} %bitcast.11, f32[3,96,96]{2,1,0:T(8,128)} %bitcast.13, ...), custom_call_target="tpu_custom_call" | custom-call | tf_op jit(solution)/shard_map/pallas_call | solution.py:784
  93.8 0.0 copy-start
  93.8 1.8 %copy.23 = f32[2,2,3,9216]{3,1,2,0:T(2,128)} copy(f32[2,2,3,9216]{3,1,2,0:T(2,128)} %bitcast.12) | data formatting | bytes 884736
  95.6 0.0 copy-done
  95.6 0.5 copy.24
Async XLA Ops:
  93.8 1.8 %copy-start = (f32[2]{0:T(128)S(1)}, f32[2]{0:T(128)}, u32[]{:S(2)}) copy-start(f32[2]{0:T(128)} %get-tuple-element.13) | copy-start | bytes 28

commit v3 on v2

--- a/solution.py
+++ b/solution.py
@@ -132,12 +132,8 @@
     bh,
     bl,
     part,
-    col,
-    csum,
     full,
     epart,
-    ecol,
-    ecsum,
     efull,
     qs,
     ob,
@@ -154,8 +150,6 @@
     r_b,
     s_g,
     r_g,
-    s_c,
-    r_c,
     s_p,
     r_p,
     s_o,
@@ -183,12 +177,11 @@
     xr = 2 * yl + mod(xl + yl, 2)
     zr = 2 * core + mod(zl + core, 2)
     place = 4 * xr + zr
-    me = 4 * mod(xr + 2 * x2, 4) + mod(zr + gz, 4)
+    me = 4 * mod(xr + 2 * x2, 4) + mod(zr + 2 * quot(gz, 2), 4)
     chip = 2 * xr + zr - 2
     is_k = both(core == 1, chip < HOLDERS)
     active = jnp.logical_or(i <= 8, i >= 24)
     lone = i == 8
-    summing = both(active, p < 7)
 
     def dev(pp, ii):
         return {"band": pp, "fft": ii}
@@ -207,7 +200,7 @@
         return at_place(y2, x2, gz, n // 4, n % 4)
 
     def slab_of(n):
-        return 4 * mod(n // 4 + 2 * x2, 4) + mod(n % 4 + gz, 4)
+        return 4 * mod(n // 4 + 2 * x2, 4) + mod(n % 4 + 2 * quot(gz, 2), 4)
 
     def is_me(where):
         return both(where["band"] == p, where["fft"] == i)
@@ -277,8 +270,7 @@
 
     def v_target(n):
         xx = mod(quot(gx, 2) + yl, 2)
-        zz = 2 * core + n
-        return at_place(y2, xx, zz, mod(gx + 2 * xx, 4), mod(quot(gzz, 2) - zz + 4, 4))
+        return at_place(y2, xx, 2 * core + n, mod(gx + 2 * xx, 4), mod(quot(gzz, 2) + 2 * core, 4))
 
     expected = jnp.int32(30)
     for k in range(6):
@@ -521,6 +513,9 @@
 
     lax.fori_loop(0, 3, step, 0)
 
+    on_zero = core == 0
+    summing = both(on_zero, active)
+
     def for_rows(do):
         @pl.when(is_k)
         def _():
@@ -530,37 +525,26 @@
 
                 @pl.when(held)
                 def _():
-                    for t in range(7):
-                        target = dev(t, home)
-                        do(a, t, jj, target)
+                    for n in range(4):
+                        do(a, n, jj, dev(2 * n, home))
 
     def scatter(src, w):
-        def one(a, t, jj, target):
-            dst = gy.at[w, pl.ds(pl.multiple_of(128 * jj + 8 * band, 8), 8)]
-            row = src.at[a, pl.ds(8 * t, 8)]
-
-            @pl.when(is_me(target))
-            def _():
-                pltpu.make_async_copy(row, dst, r_g.at[w]).start()
-
-            @pl.when(jnp.logical_not(is_me(target)))
-            def _():
-                remote(row, dst, s_g.at[w, 7 * a + t], r_g.at[w], target).start()
+        def one(a, n, jj, target):
+            dst = gy.at[w, pl.ds(pl.multiple_of(256 * jj + 16 * band, 8), 16)]
+            remote(src.at[a, pl.ds(16 * n, 16)], dst, s_g.at[w, 4 * a + n], r_g.at[w], target).start()
 
         for_rows(one)
 
     def scattered(src, w):
-        def one(a, t, jj, target):
-            @pl.when(jnp.logical_not(is_me(target)))
-            def _():
-                await_bytes(src.at[a, pl.ds(8 * t, 8)], s_g.at[w, 7 * a + t])
+        def one(a, n, jj, target):
+            await_bytes(src.at[a, pl.ds(16 * n, 16)], s_g.at[w, 4 * a + n])
 
         for_rows(one)
 
     def all_rows(w):
         @pl.when(lone)
         def _():
-            await_bytes(gy.at[w, pl.ds(0, 128)], r_g.at[w])
+            await_bytes(gy.at[w, pl.ds(0, 256)], r_g.at[w])
 
         @pl.when(jnp.logical_not(lone))
         def _():
@@ -568,8 +552,8 @@
 
         rows = []
         for jj in range(3):
-            for r in range(8):
-                x = gy[w, pl.ds(128 * jj + r, BANDS, stride=8), :]
+            for r in range(16):
+                x = gy[w, pl.ds(256 * jj + r, BANDS, stride=16), :]
                 rows.append(jnp.where(lone, 0.0, x) if jj else x)
         a = jnp.concatenate(rows, axis=1)
         b = jnp.concatenate([-sign * swap(x) for x in rows], axis=1)
@@ -577,47 +561,10 @@
 
     my_slot = jnp.minimum(jnp.where(i <= 8, i, jnp.maximum(i - 15, 0)), 16)
 
-    def column_send(w, mine, theirs):
-        for t in range(8):
-
-            @pl.when(p != t)
-            def _():
-                remote(mine, theirs.at[p], s_c.at[w], r_c.at[w], dev(t, i)).start()
-
-    def column_sum(w, theirs):
-        @pl.when(p < 7)
-        def _():
-            await_bytes(theirs.at[pl.ds(0, 6)], r_c.at[w])
-
-        @pl.when(p == 7)
-        def _():
-            await_bytes(theirs.at[pl.ds(0, 7)], r_c.at[w])
-
-        total = theirs[0]
-        for t in range(1, 7):
-            total = total + theirs[t]
-        return total
-
-    def plane_send(w, mine, theirs, targets):
-        for ii in targets:
-
-            @pl.when(i != ii)
-            def _():
-                remote(mine, theirs.at[my_slot], s_p.at[w], r_p.at[w], dev(p, ii)).start()
-
-    def plane_sum(w, theirs):
-        @pl.when(active)
-        def _():
-            await_bytes(theirs.at[pl.ds(0, 16)], r_p.at[w])
-
-        @pl.when(jnp.logical_not(active))
-        def _():
-            await_bytes(theirs.at[pl.ds(0, 17)], r_p.at[w])
-
-        total = theirs[0]
-        for n in range(1, 17):
-            total = total + theirs[n]
-        return total
+    def added(terms):
+        while len(terms) > 1:
+            terms = [a + b for a, b in zip(terms[::2], terms[1::2])] + ([terms[-1]] if len(terms) % 2 else [])
+        return terms[0]
 
     lane2 = lax.broadcasted_iota(jnp.int32, (16, 128), 1)
 
@@ -641,6 +588,12 @@
     forward()
     middle(False)
 
+    def keep(a, h):
+        hy[a] = h
+
+    backward(keep)
+    scatter(hy, 1)
+
     @pl.when(summing)
     def _():
         high, low = split(all_rows(0))
@@ -652,72 +605,69 @@
         for n in range(1, 4):
             packed = packed + pltpu.roll(g[4 * n : 4 * n + 4], 32 * n, 1)
         part[...] = packed
-        col[p] = packed
-        column_send(0, part, col)
+        full[17 * y + my_slot] = packed
+        for n in range(4):
+            for ii in ACTIVE:
+
+                @pl.when(jnp.logical_not(is_me(dev(2 * n, ii))))
+                def _():
+                    remote(
+                        part, full.at[17 * y + my_slot], s_p.at[0], r_p.at[0], dev(2 * n, ii)
+                    ).start()
+
+        await_bytes(full.at[pl.ds(0, 67)], r_p.at[0])
+        total = added([full[n] for n in range(68)])
+
+        g = jnp.concatenate([total] + [pltpu.roll(total, 128 - 32 * n, 1) for n in range(1, 4)], axis=0)
+        u_rows = inverse_rows(jnp.where(lane2 < 32, g, 0.0))
+        w_high, w_low = split(jnp.where(lane2 < 16, u_rows, -u_rows)[:, :32])
+
+        def rotated(high, low):
+            return dot(w_high, high) + dot(w_high, low) + dot(w_low, high)
+
+        q = rotated(bh[...], bl[...])
+        for n in range(48):
+            qs[pl.ds(n, BANDS, stride=48), :] = q[:, 128 * n : 128 * n + 128]
+        hq = rotated(*split(all_rows(1)))
+        e = q[:, :128] * hq[:, :128]
+        for n in range(1, 48):
+            e = e + q[:, 128 * n : 128 * n + 128] * hq[:, 128 * n : 128 * n + 128]
+        e = jnp.sum(e, axis=1, keepdims=True) * (1.0 / CELLS)
+        row = lax.broadcasted_iota(jnp.int32, (16, 128), 0)
+        epart[...] = jnp.sum(jnp.where(lane2 == row, e, 0.0), axis=0, keepdims=True)
+        mine = 17 * y + my_slot
+        efull[mine] = epart[...]
+        for pp in range(8):
+            for n in range(32):
+                ii = mod(i + 4 + n, 32)
+
+                def send():
+                    remote(epart, efull.at[mine], s_p.at[1], r_p.at[1], dev(pp, ii)).start()
+
+                if n == 28:
+                    pl.when(p != pp)(send)
+                else:
+                    send()
+
+        for t in range(8):
+            src = qs.at[pl.ds(96 * t, 96)]
+
+            @pl.when(p == t)
+            def _():
+                pltpu.make_async_copy(src, ob.at[y], r_o.at[0]).start()
+
+            @pl.when(p != t)
+            def _():
+                remote(src, ob.at[y], s_o.at[t], r_o.at[0], dev(t, i)).start()
 
     @pl.when(active)
     def _():
-        total = column_sum(0, col)
-        csum[...] = total
-        full[my_slot] = total
-        plane_send(0, csum, full, ACTIVE)
-
-    def keep(a, h):
-        hy[a] = h
-
-    backward(keep)
-    scatter(hy, 1)
-
-    @pl.when(active)
-    def _():
-        total = plane_sum(0, full)
-
-        @pl.when(p < 7)
-        def _():
-            g = jnp.concatenate([total] + [pltpu.roll(total, 128 - 32 * n, 1) for n in range(1, 4)], axis=0)
-            u = inverse_rows(jnp.where(lane2 < 32, g, 0.0))
-            w_high, w_low = split(jnp.where(lane2 < 16, u, -u)[:, :32])
-
-            def rotated(high, low):
-                return dot(w_high, high) + dot(w_high, low) + dot(w_low, high)
-
-            q = rotated(bh[...], bl[...])
-            for n in range(24):
-                qs[pl.ds(n, BANDS, stride=24), :] = q[:, 128 * n : 128 * n + 128]
-
-            for t in range(8):
-                src = qs.at[pl.ds(48 * t, 48)]
-
-                @pl.when(p == t)
-                def _():
-                    pltpu.make_async_copy(src, ob.at[p], r_o.at[0]).start()
-
-                @pl.when(p != t)
-                def _():
-                    remote(src, ob.at[p], s_o.at[0], r_o.at[0], dev(t, i)).start()
-
-            hq = rotated(*split(all_rows(1)))
-            e = q[:, :128] * hq[:, :128]
-            for n in range(1, 24):
-                e = e + q[:, 128 * n : 128 * n + 128] * hq[:, 128 * n : 128 * n + 128]
-            e = jnp.sum(e, axis=1, keepdims=True) * (1.0 / CELLS)
-            row = lax.broadcasted_iota(jnp.int32, (16, 128), 0)
-            e = jnp.sum(jnp.where(lane2 == row, e, 0.0), axis=0, keepdims=True)
-            epart[...] = e
-            ecol[p] = e
-            column_send(1, epart, ecol)
-
-        total = column_sum(1, ecol)
-        ecsum[...] = total
-        efull[my_slot] = total
-        plane_send(1, ecsum, efull, range(32))
-
         await_bytes(ob, r_o.at[0])
-        zero = jnp.zeros((72, 128), F32)
+        zero = jnp.zeros((64, 128), F32)
         low_lanes, high_lanes = lane < 25, jnp.logical_and(lane >= 72, lane < 96)
         for k in range(6):
             j, jj = k // 3, k % 3
-            rows = jnp.concatenate([ob[t, 8 * k : 8 * k + 8, :] for t in range(7)] + [zero], axis=0)
+            rows = jnp.concatenate([ob[n, 16 * k : 16 * k + 16, :] for n in range(4)] + [zero], axis=0)
             if jj:
                 rows = jnp.where(lone, 0.0, rows)
             rows = rows.T
@@ -754,27 +704,35 @@
 
     @pl.when(summing)
     def _():
-        await_bytes(col.at[pl.ds(0, 7)], s_c.at[0])
-        await_bytes(ecol.at[pl.ds(0, 7)], s_c.at[1])
-        await_bytes(qs.at[pl.ds(0, 48 * 7)], s_o.at[0])
-
-    @pl.when(active)
+        await_bytes(sbuf.at[0, pl.ds(0, 255)], s_p.at[1])
+        await_bytes(full.at[pl.ds(0, 67)], s_p.at[0])
+        for t in range(8):
+
+            @pl.when(p != t)
+            def _():
+                await_bytes(qs.at[pl.ds(96 * t, 96)], s_o.at[t])
+
+    await_bytes(xin, s_out.at[0])
+
+    @pl.when(summing)
     def _():
-        await_bytes(full.at[pl.ds(0, 16)], s_p.at[0])
-        await_bytes(efull.at[pl.ds(0, 31)], s_p.at[1])
-
-    await_bytes(xin, s_out.at[0])
-
-    e = plane_sum(1, efull)
-    for j in range(2):
-        energy_ref[j] = jnp.sum(jnp.where(lane == 2 * p + j, e, 0.0))
+        await_bytes(efull.at[pl.ds(0, 67)], r_p.at[1])
+
+    @pl.when(jnp.logical_not(summing))
+    def _():
+        await_bytes(efull, r_p.at[1])
+
+    e = added([efull[n] for n in range(68)])
+    energy_ref[...] = pltpu.roll(e, 128 - 2 * p, 1)[:, :2]
     weights = jax.nn.sigmoid((fermi_ref[0] - e) / TEMPER)
-    band_energy_ref[0] = jnp.sum(jnp.where(lane < BANDS, weights * e, 0.0)) / float(BANDS)
+    weighted = jnp.where(lane < BANDS, weights * e, 0.0)
+    band_energy_ref[...] = jnp.sum(weighted, axis=1, keepdims=True) / float(BANDS)
 
 
 def call(lower, upper, fermi, height, x, v):
     smem = pl.BlockSpec(memory_space=pltpu.SMEM)
     hbm = pl.BlockSpec(memory_space=pl.ANY)
+    vmem = pl.BlockSpec(memory_space=pltpu.VMEM)
     sem = pltpu.SemaphoreType.DMA
     consts = tables()
 
@@ -785,11 +743,11 @@
         kernel,
         out_shape=(
             jax.ShapeDtypeStruct((6, 144, 128), F32),
-            jax.ShapeDtypeStruct((2,), F32),
-            jax.ShapeDtypeStruct((1,), F32),
+            jax.ShapeDtypeStruct((1, 2), F32),
+            jax.ShapeDtypeStruct((1, 1), F32),
         ),
         in_specs=[smem] * 3 + [hbm] * 9,
-        out_specs=(hbm, smem, smem),
+        out_specs=(hbm, vmem, vmem),
         scratch_shapes=[
             buf(6, 144, 128),
             buf(2, 96, 128),
@@ -811,37 +769,31 @@
             buf(2, 7, 24, 128),
             buf(2, 7, 24, 128),
             buf(2, 384, 128),
-            buf(2, 384, 128),
-            pltpu.VMEM((32, 3072), BF16),
-            pltpu.VMEM((32, 3072), BF16),
+            buf(2, 768, 128),
+            pltpu.VMEM((32, 6144), BF16),
+            pltpu.VMEM((32, 6144), BF16),
             buf(4, 128),
-            buf(8, 4, 128),
-            buf(4, 128),
-            buf(17, 4, 128),
+            buf(68, 4, 128),
             buf(1, 128),
-            buf(8, 1, 128),
-            buf(1, 128),
-            buf(32, 1, 128),
-            buf(384, 128),
-            buf(7, 48, 128),
+            buf(68, 1, 128),
+            buf(768, 128),
+            buf(4, 96, 128),
             sem((3,)),
             sem((1,)),
             sem((6,)),
             sem((6,)),
             sem((8,)),
+            sem((4,)),
             sem((2,)),
             sem((2,)),
             sem((2,)),
             sem((2,)),
             sem((2,)),
-            sem((2,)),
-            sem((2, 56)),
+            sem((2, 32)),
             sem((2,)),
             sem((2,)),
             sem((2,)),
-            sem((2,)),
-            sem((2,)),
-            sem((1,)),
+            sem((8,)),
             sem((1,)),
             pltpu.SemaphoreType.REGULAR,
         ],
@@ -856,7 +808,7 @@
     v = potential.transpose(2, 0, 1)
     out, energies, band_energy = call(lower_bound, upper_bound, fermi_level, half_height, x, v)
     out = out.reshape(2, 3, 72, 2, 128).transpose(0, 3, 1, 2, 4).reshape(2, 2, 3, NG * NG)
-    return out, energies, band_energy
+    return out, energies.reshape(2), band_energy.reshape(1)
 
 
 def solution(mesh):

time: 98 us -> 97.6 us (level)
  no operation moved by 1% of the time
where the time goes in v3:
time: 97.6 us; the launch traced here: 97.4 us
  Pallas kernels  90.8 us (93%)
  between operations  4.35 us (4%)
  local copies, waits for them, and re-layouts  2.32 us (2%)
    pallas_call x1, Pallas kernels, call(): pl.pallas_call(kernel, out_shape=(jax.ShapeDtypeStruct((6, 144, 128), F32...  90.8 us
    unnamed x4, local copies, waits for them, and re-layouts  2.32 us

profile of v3, /device:TPU:1, one launch (start us, length us, event | category | flops | bytes accessed | tf_op | source)
XLA Modules:
  0.0 97.4 jit_solution(16746283071287500309)
XLA Ops:
  2.6 90.8 %shard_map.139 = (f32[6,144,128]{2,1,0:T(8,128)}, f32[1,2]{1,0:T(1,128)}, f32[1,1]{1,0:T(1,128)}) custom-call(f32[1]{0:T(128)S(6)} %copy.20.lower_ref, f32[1]{0:T(128)S(6)} %copy.21.upper_ref, f32[1]{0:T(128)S(6)} %copy.22.fermi_ref, s32[3,96]{1,0:T(4,128)} %height_hbm.1, f32[6,144,128]{2,1,0:T(8,128)} %bitcast.13, f32[3,96,96]{2,1,0:T(8,128)} %bitcast.15, ...), custom_call_target="tpu_custom_call" | custom-call | tf_op jit(solution)/shard_map/pallas_call | solution.py:742
  93.4 0.0 copy-start
  93.4 1.8 %copy.23 = f32[2,2,3,9216]{3,1,2,0:T(2,128)} copy(f32[2,2,3,9216]{3,1,2,0:T(2,128)} %bitcast.14) | data formatting | bytes 884736
  95.2 0.0 copy-done
  95.2 0.5 copy.24
Async XLA Ops:
  93.4 1.8 %copy-start = (f32[1,2]{1,0:T(1,128)S(1)}, f32[1,2]{1,0:T(1,128)}, u32[]{:S(2)}) copy-start(f32[1,2]{1,0:T(1,128)} %get-tuple-element.7) | copy-start | bytes 28

commit v4 on v3

--- a/solution.py
+++ b/solution.py
@@ -15,6 +15,7 @@
 KIN = 12.0 / 24**2
 TEMPER = 0.5
 BANDS = 16
+FAR_FIRST = (7, 6, 5, 3, 4, 2, 1, 0)
 ACTIVE = (*range(9), *range(24, 32))
 MEMBERS = 16
 HOLDERS = 7
@@ -199,8 +200,13 @@
     def mine_at(n):
         return at_place(y2, x2, gz, n // 4, n % 4)
 
-    def slab_of(n):
-        return 4 * mod(n // 4 + 2 * x2, 4) + mod(n % 4 + 2 * quot(gz, 2), 4)
+    def across(d, c):
+        yy, xx, zz = mod(yl + d // 4, 2), mod(xl + d // 2 % 2, 2), mod(zl + d % 2, 2)
+        return (
+            2 * yy + mod(xx + yy, 2),
+            2 * c + mod(zz + c, 2),
+            dev(4 * y2 + 2 * yy + c, 16 * x2 + 8 * xx + 2 * gz + zz),
+        )
 
     def is_me(where):
         return both(where["band"] == p, where["fft"] == i)
@@ -408,17 +414,16 @@
                     c, s = out[:48, 128 * a : 128 * a + 128], out[48:, 128 * a : 128 * a + 128]
                     sbuf[h, pl.ds(a, 48, stride=8), :] = c + sign * swap(s)
 
-                for n in range(MEMBERS):
-                    src = sbuf.at[h, message(slab_of(n))]
-                    home = rbuf.at[h, chip]
-
-                    @pl.when(place == n)
-                    def _():
-                        pltpu.make_async_copy(src, home, r_f.at[h]).start()
-
-                    @pl.when(place != n)
-                    def _():
-                        remote(src, home, s_f.at[h], r_f.at[h], mine_at(n)).start()
+                home = rbuf.at[h, chip]
+                for d in FAR_FIRST:
+                    for c in range(2):
+                        xr_, zr_, target = across(d, c)
+                        slab = 4 * mod(xr_ + 2 * x2, 4) + mod(zr_ + 2 * quot(gz, 2), 4)
+                        src = sbuf.at[h, message(slab)]
+                        if d == 0 and c == 1:
+                            pltpu.make_async_copy(src, home, r_f.at[h]).start()
+                        else:
+                            remote(src, home, s_f.at[h], r_f.at[h], target).start()
 
     def middle(first):
         zero8 = jnp.zeros((8, 128), F32)
@@ -461,17 +466,23 @@
                 for s in range(HOLDERS):
                     bbuf[h, s, 8 * z : 8 * z + 8, :] = o[8 * s : 8 * s + 8]
 
-            for s in range(HOLDERS):
-                home = kbuf.at[h, message(me)]
-                mine = both(is_k, chip == s)
-
-                @pl.when(mine)
+            home = kbuf.at[h, message(me)]
+            for d in FAR_FIRST:
+                xr_, zr_, target = across(d, 1)
+                s = 2 * xr_ + zr_ - 2
+                src = bbuf.at[h, jnp.minimum(s, HOLDERS - 1)]
+                held = s < HOLDERS
+                if d == 0:
+
+                    @pl.when(is_k)
+                    def _():
+                        pltpu.make_async_copy(src, home, r_b.at[h]).start()
+
+                    held = both(held, core == 0)
+
+                @pl.when(held)
                 def _():
-                    pltpu.make_async_copy(bbuf.at[h, s], home, r_b.at[h]).start()
-
-                @pl.when(jnp.logical_not(mine))
-                def _():
-                    remote(bbuf.at[h, s], home, s_b.at[h], r_b.at[h], mine_at(4 * (s // 2) + 2 + s % 2)).start()
+                    remote(src, home, s_b.at[h], r_b.at[h], target).start()
 
     def backward(finish):
         @pl.when(is_k)

time: 97.6 us -> 95.7 us (0.981)
  Pallas kernels: 90.8 us -> 88.8 us
    pallas_call x1, Pallas kernels: 90.8 us -> 88.8 us  [call(): pl.pallas_call(kernel, out_shape=(jax.ShapeDtypeStruct((6, 144, 128), F32...]
where the time goes in v4:
time: 95.7 us; the launch traced here: 95.5 us
  Pallas kernels  88.8 us (93%)
  between operations  4.35 us (5%)
  local copies, waits for them, and re-layouts  2.32 us (2%)
    pallas_call x1, Pallas kernels, call(): pl.pallas_call(kernel, out_shape=(jax.ShapeDtypeStruct((6, 144, 128), F32...  88.8 us
    unnamed x4, local copies, waits for them, and re-layouts  2.32 us

profile of v4, /device:TPU:1, one launch (start us, length us, event | category | flops | bytes accessed | tf_op | source)
XLA Modules:
  0.0 95.5 jit_solution(16709227724565676179)
XLA Ops:
  2.6 88.8 %shard_map.139 = (f32[6,144,128]{2,1,0:T(8,128)}, f32[1,2]{1,0:T(1,128)}, f32[1,1]{1,0:T(1,128)}) custom-call(f32[1]{0:T(128)S(6)} %copy.20.lower_ref, f32[1]{0:T(128)S(6)} %copy.21.upper_ref, f32[1]{0:T(128)S(6)} %copy.22.fermi_ref, s32[3,96]{1,0:T(4,128)} %height_hbm.1, f32[6,144,128]{2,1,0:T(8,128)} %bitcast.13, f32[3,96,96]{2,1,0:T(8,128)} %bitcast.15, ...), custom_call_target="tpu_custom_call" | custom-call | tf_op jit(solution)/shard_map/pallas_call | solution.py:753
  91.4 0.0 copy-start
  91.4 1.8 %copy.23 = f32[2,2,3,9216]{3,1,2,0:T(2,128)} copy(f32[2,2,3,9216]{3,1,2,0:T(2,128)} %bitcast.14) | data formatting | bytes 884736
  93.2 0.0 copy-done
  93.2 0.5 copy.24
Async XLA Ops:
  91.4 1.8 %copy-start = (f32[1,2]{1,0:T(1,128)S(1)}, f32[1,2]{1,0:T(1,128)}, u32[]{:S(2)}) copy-start(f32[1,2]{1,0:T(1,128)} %get-tuple-element.7) | copy-start | bytes 28

commit v5 on v4

--- a/solution.py
+++ b/solution.py
@@ -15,6 +15,10 @@
 KIN = 12.0 / 24**2
 TEMPER = 0.5
 BANDS = 16
+OFFSETS = sorted(
+    ((dy, dx, dz) for dy in range(4) for dx in range(4) for dz in range(8)),
+    key=lambda d: -(min(d[0], 4 - d[0]) + min(d[1], 4 - d[1]) + min(d[2], 8 - d[2])),
+)
 FAR_FIRST = (7, 6, 5, 3, 4, 2, 1, 0)
 ACTIVE = (*range(9), *range(24, 32))
 MEMBERS = 16
@@ -617,14 +621,17 @@
             packed = packed + pltpu.roll(g[4 * n : 4 * n + 4], 32 * n, 1)
         part[...] = packed
         full[17 * y + my_slot] = packed
-        for n in range(4):
+        for dy in (2, 1, 3, 0):
+            pp = 2 * mod(y + dy, 4)
             for ii in ACTIVE:
 
-                @pl.when(jnp.logical_not(is_me(dev(2 * n, ii))))
-                def _():
-                    remote(
-                        part, full.at[17 * y + my_slot], s_p.at[0], r_p.at[0], dev(2 * n, ii)
-                    ).start()
+                def send():
+                    remote(part, full.at[17 * y + my_slot], s_p.at[0], r_p.at[0], dev(pp, ii)).start()
+
+                if dy:
+                    send()
+                else:
+                    pl.when(i != ii)(send)
 
         await_bytes(full.at[pl.ds(0, 67)], r_p.at[0])
         total = added([full[n] for n in range(68)])
@@ -648,17 +655,10 @@
         epart[...] = jnp.sum(jnp.where(lane2 == row, e, 0.0), axis=0, keepdims=True)
         mine = 17 * y + my_slot
         efull[mine] = epart[...]
-        for pp in range(8):
-            for n in range(32):
-                ii = mod(i + 4 + n, 32)
-
-                def send():
-                    remote(epart, efull.at[mine], s_p.at[1], r_p.at[1], dev(pp, ii)).start()
-
-                if n == 28:
-                    pl.when(p != pp)(send)
-                else:
-                    send()
+        for dy, dx, dz in OFFSETS:
+            pp, ii = 2 * mod(y + dy, 4), 8 * mod(gx + dx, 4) + mod(gzz + dz, 8)
+            for c in range(1 if dy + dx + dz == 0 else 0, 2):
+                remote(epart, efull.at[mine], s_p.at[1], r_p.at[1], dev(pp + c, ii)).start()
 
         for t in range(8):
             src = qs.at[pl.ds(96 * t, 96)]

time: 95.7 us -> 94.9 us (level)
  no operation moved by 1% of the time
where the time goes in v5:
time: 94.9 us; the launch traced here: 94.7 us
  Pallas kernels  88 us (93%)
  between operations  4.35 us (5%)
  local copies, waits for them, and re-layouts  2.32 us (2%)
    pallas_call x1, Pallas kernels, call(): pl.pallas_call(kernel, out_shape=(jax.ShapeDtypeStruct((6, 144, 128), F32...  88 us
    unnamed x4, local copies, waits for them, and re-layouts  2.32 us

profile of v5, /device:TPU:1, one launch (start us, length us, event | category | flops | bytes accessed | tf_op | source)
XLA Modules:
  0.0 94.7 jit_solution(4096404594623243724)
XLA Ops:
  2.6 88.0 %shard_map.139 = (f32[6,144,128]{2,1,0:T(8,128)}, f32[1,2]{1,0:T(1,128)}, f32[1,1]{1,0:T(1,128)}) custom-call(f32[1]{0:T(128)S(6)} %copy.20.lower_ref, f32[1]{0:T(128)S(6)} %copy.21.upper_ref, f32[1]{0:T(128)S(6)} %copy.22.fermi_ref, s32[3,96]{1,0:T(4,128)} %height_hbm.1, f32[6,144,128]{2,1,0:T(8,128)} %bitcast.13, f32[3,96,96]{2,1,0:T(8,128)} %bitcast.15, ...), custom_call_target="tpu_custom_call" | custom-call | tf_op jit(solution)/shard_map/pallas_call | solution.py:753
  90.6 0.0 copy-start
  90.6 1.8 %copy.23 = f32[2,2,3,9216]{3,1,2,0:T(2,128)} copy(f32[2,2,3,9216]{3,1,2,0:T(2,128)} %bitcast.14) | data formatting | bytes 884736
  92.4 0.0 copy-done
  92.4 0.5 copy.24
Async XLA Ops:
  90.6 1.8 %copy-start = (f32[1,2]{1,0:T(1,128)S(1)}, f32[1,2]{1,0:T(1,128)}, u32[]{:S(2)}) copy-start(f32[1,2]{1,0:T(1,128)} %get-tuple-element.7) | copy-start | bytes 28
